TPU v7x, 256 devices: a whole 4x4x8 slice. The times are simulated.
256 devices in a mesh: depth: 32 (over z, y), batch: 8 (over x, core).
Axes of the slice: x: 4, y: 4, z: 8, core: 2. Of those that a mesh axis runs over, the one named last changes fastest.
Arguments:
- iterate: float32 [32, 16, 16, 16, 256], P('depth', 'batch'), may hold values from -70 to 70
- weights: bfloat16 [128, 3, 3, 256, 256], P('depth'), may hold values from -0.125 to 0.125
- norm_scale: float32 [128, 256], P('depth'), may hold values from 0.5 to 2
- norm_shift: float32 [128, 256], P('depth'), may hold values from -3 to 3
Outputs:
- block_ends: float32 [32, 16, 16, 16, 256], P('depth', 'batch')
All inputs are finite; a program needn't handle non-finite values.
Results may differ from a plain program's by a relative error of at most 0.0018.
Values sent between devices are 32-bit elements; how exact they have to be, the bound alone decides.
A program may use at most 64 MiB of HBM per device.

v0:
```python
import functools

import jax
import jax.numpy as jnp
from jax import lax
from jax.sharding import Mesh
from jax.sharding import PartitionSpec as P

BATCH = ("batch_0", "batch_1")


fine_step = 0.125
coarse_step = 0.5
epsilon = 1e-05


def by_axis(shard, axes):
    return functools.reduce(lax.psum, axes, shard)


def passed_along(block, axis, distance):
    devices = range(lax.axis_size(axis))
    route = [(i - distance, i) for i in devices if i - distance in devices]
    return lax.ppermute(block, axis, route)


def convolve(activated, kernel):
    return lax.conv_general_dilated(
        activated,
        kernel,
        (1, 1),
        "SAME",
        dimension_numbers=("NHWC", "HWIO", "NHWC"),
        preferred_element_type=jnp.float32,
    )


def activate(current, gain_row, offset, center, inverse):
    return jax.nn.relu(gain_row * (current - center) * inverse + offset).astype(jnp.bfloat16)


def fine_layer(current, kernel, gain_row, offset):
    totals = (jnp.sum(current, axis=(0, 1, 2)), jnp.sum(current * current, axis=(0, 1, 2)))
    plain_sum, square_sum = (by_axis(totals[0], BATCH), by_axis(totals[1], BATCH))
    entries = current.shape[0] * current.shape[1] * current.shape[2] * lax.axis_size(BATCH)
    center = plain_sum / entries
    inverse = lax.rsqrt(square_sum / entries - center * center + epsilon)
    activated = activate(current, gain_row, offset, center, inverse)
    return (current + fine_step * convolve(activated, kernel), center, inverse)


def shards(iterate, weights, norm_scale, norm_shift):
    initial = iterate[0]
    position = lax.axis_index("depth")
    devices = lax.axis_size("depth")
    current = initial
    for number in range(4):
        current, center, inverse = fine_layer(
            current, weights[number], norm_scale[number], norm_shift[number]
        )
    arrived = passed_along(current, "depth", 1)
    begin_state = jnp.where(position == 0, initial, arrived)
    current = begin_state
    first_center = None
    first_inverse = None
    for number in range(4):
        current, center, inverse = fine_layer(
            current, weights[number], norm_scale[number], norm_shift[number]
        )
        if number == 0:
            first_center, first_inverse = (center, inverse)

    def coarse(incoming):
        activated = activate(incoming, norm_scale[0], norm_shift[0], first_center, first_inverse)
        return incoming + coarse_step * convolve(activated, weights[0])

    forcing = current - coarse(begin_state)
    samples = initial.shape[0]

    def advance(step_id, carried):
        incoming, block_ends = carried
        sample = step_id - position
        active_turn = (sample >= 0) & (sample < samples)
        slot_at = jnp.clip(sample, 0, samples - 1)
        taken_in = lax.dynamic_slice_in_dim(incoming, slot_at, 1, 0)
        forcing_at = lax.dynamic_slice_in_dim(forcing, slot_at, 1, 0)
        produced = lax.cond(
            active_turn,
            lambda operands: coarse(operands[0]) + operands[1],
            lambda operands: jnp.zeros_like(operands[0]),
            (taken_in, forcing_at),
        )
        block_ends = jnp.where(
            active_turn,
            lax.dynamic_update_slice_in_dim(block_ends, produced, slot_at, 0),
            block_ends,
        )
        passed = passed_along(produced, "depth", 1)
        target = sample + 1
        landing = (position > 0) & (target >= 0) & (target < samples)
        place_at = jnp.clip(target, 0, samples - 1)
        incoming = jnp.where(
            landing, lax.dynamic_update_slice_in_dim(incoming, passed, place_at, 0), incoming
        )
        return (incoming, block_ends)

    incoming, block_ends = lax.fori_loop(
        0, devices + samples - 1, advance, (initial, jnp.zeros_like(initial))
    )
    return block_ends[None]


def solution(mesh):
    finer = Mesh(mesh.devices.reshape(mesh.shape["depth"], 4, 2), ("depth", "batch_0", "batch_1"))
    return jax.shard_map(
        shards,
        mesh=finer,
        in_specs=(
            P("depth", BATCH, None, None, None),
            P("depth", None, None, None, None),
            P("depth", None),
            P("depth", None),
        ),
        out_specs=P("depth", BATCH, None, None, None),
        check_vma=False,
    )
```

profile of v0, /device:TPU:130, one launch (start us, length us, event | category | flops | bytes accessed | tf_op | source)
XLA Modules:
  0.0 559.4 jit_solution(11239392886545528639)
XLA Ops:
  4.2 8.6 %all-reduce.7 = (f32[256]{0:T(256)S(1)}, f32[256]{0:T(256)S(1)}) all-reduce(f32[256]{0:T(256)S(1)} %multiply_reduce_fusion.7, f32[256]{0:T(256)S(1)} %reduce_sum.144), channel_id=1, replica_groups=mesh['depth'=32,'batch_0'=4,'batch_1'=2] {'batch_0'}, use_global_device_ids=true, to_apply=%region_4.0 | all-reduce | flops 512 | bytes 4096 | tf_op jit(solution)/shard_map/psum | solution.py:18
  12.8 2.5 all-reduce.15
  16.2 2.4 fusion.31
  19.4 10.1 %all-reduce.6 = (f32[256]{0:T(256)S(1)}, f32[256]{0:T(256)S(1)}) all-reduce(f32[256]{0:T(256)S(1)} %get-tuple-element.306, f32[256]{0:T(256)S(1)} %get-tuple-element.305), channel_id=1, replica_groups=mesh['depth'=32,'batch_0'=4,'batch_1'=2] {'batch_0'}, use_global_device_ids=true, to_apply=%region_10.11 | all-reduce | flops 512 | bytes 4096 | tf_op jit(solution)/shard_map/psum | solution.py:18
  29.5 2.5 all-reduce.14
  32.2 2.4 fusion.30
  35.2 7.8 %all-reduce.5 = (f32[256]{0:T(256)S(1)}, f32[256]{0:T(256)S(1)}) all-reduce(f32[256]{0:T(256)S(1)} %get-tuple-element.304, f32[256]{0:T(256)S(1)} %get-tuple-element.303), channel_id=1, replica_groups=mesh['depth'=32,'batch_0'=4,'batch_1'=2] {'batch_0'}, use_global_device_ids=true, to_apply=%region_16.17 | all-reduce | flops 512 | bytes 4096 | tf_op jit(solution)/shard_map/psum | solution.py:18
  43.0 2.5 all-reduce.13
  45.7 2.4 fusion.29
  48.6 9.8 %all-reduce.4 = (f32[256]{0:T(256)S(1)}, f32[256]{0:T(256)S(1)}) all-reduce(f32[256]{0:T(256)S(1)} %get-tuple-element.302, f32[256]{0:T(256)S(1)} %get-tuple-element.301), channel_id=1, replica_groups=mesh['depth'=32,'batch_0'=4,'batch_1'=2] {'batch_0'}, use_global_device_ids=true, to_apply=%region_22.23 | all-reduce | flops 512 | bytes 4096 | tf_op jit(solution)/shard_map/psum | solution.py:18
  58.4 2.5 all-reduce.12
  61.1 2.4 fusion.28
  64.0 3.5 collective-permute-start.1
  67.8 15.4 %collective-permute-done.1 = f32[2,16,16,256]{3,1,2,0:T(8,128)S(1)} collective-permute-done((f32[2,16,16,256]{3,1,2,0:T(8,128)S(1)}, f32[2,16,16,256]{3,1,2,0:T(8,128)S(1)}, u32[]{:S(2)}, u32[]{:S(2)}) %collective-permute-start.1) | collective-permute-done | bytes 524320 | tf_op jit(solution)/shard_map/ppermute | solution.py:24
  83.6 7.7 %all-reduce.3 = (f32[256]{0:T(256)S(1)}, f32[256]{0:T(256)S(1)}) all-reduce(f32[256]{0:T(256)S(1)} %get-tuple-element.300, f32[256]{0:T(256)S(1)} %get-tuple-element.299), channel_id=1, replica_groups=mesh['depth'=32,'batch_0'=4,'batch_1'=2] {'batch_0'}, use_global_device_ids=true, to_apply=%region_25.26 | all-reduce | flops 512 | bytes 4096 | tf_op jit(solution)/shard_map/psum | solution.py:18
  91.3 2.5 all-reduce.11
  94.0 2.4 broadcast_multiply_fusion.1
  97.0 9.7 %all-reduce.2 = (f32[256]{0:T(256)S(1)}, f32[256]{0:T(256)S(1)}) all-reduce(f32[256]{0:T(256)S(1)} %get-tuple-element.298, f32[256]{0:T(256)S(1)} %get-tuple-element.297), channel_id=1, replica_groups=mesh['depth'=32,'batch_0'=4,'batch_1'=2] {'batch_0'}, use_global_device_ids=true, to_apply=%region_34.35 | all-reduce | flops 512 | bytes 4096 | tf_op jit(solution)/shard_map/psum | solution.py:18
  106.7 2.6 all-reduce.10
  109.6 2.4 fusion.27
  112.6 7.8 %all-reduce.1 = (f32[256]{0:T(256)S(1)}, f32[256]{0:T(256)S(1)}) all-reduce(f32[256]{0:T(256)S(1)} %get-tuple-element.296, f32[256]{0:T(256)S(1)} %get-tuple-element.295), channel_id=1, replica_groups=mesh['depth'=32,'batch_0'=4,'batch_1'=2] {'batch_0'}, use_global_device_ids=true, to_apply=%region_40.41 | all-reduce | flops 512 | bytes 4096 | tf_op jit(solution)/shard_map/psum | solution.py:18
  120.3 2.5 all-reduce.9
  123.0 2.4 fusion.26
  126.0 9.7 %all-reduce = (f32[256]{0:T(256)S(1)}, f32[256]{0:T(256)S(1)}) all-reduce(f32[256]{0:T(256)S(1)} %get-tuple-element.294, f32[256]{0:T(256)S(1)} %get-tuple-element.293), channel_id=1, replica_groups=mesh['depth'=32,'batch_0'=4,'batch_1'=2] {'batch_0'}, use_global_device_ids=true, to_apply=%region_46.47 | all-reduce | flops 512 | bytes 4096 | tf_op jit(solution)/shard_map/psum | solution.py:18
  135.8 2.5 all-reduce.8
  138.5 2.4 fusion.25
  142.0 416.6 %while.16 = (s32[]{:T(128)}, f32[2,16,16,256]{3,1,2,0:T(8,128)S(1)}, f32[2,16,16,256]{3,2,1,0:T(8,128)S(1)}, s32[]{:T(128)}, pred[]{:T(512)}, /*index=5*/f32[4,2...) while((s32[]{:T(128)}, ...), condition=%wide.region_51.52_spmd, body=%wide.region_48.51_spmd.sunk | while | flops 435945472 | bytes 8741403 | solution.py:107
  144.4 11.3 %collective-permute-done = f32[1,16,16,256]{3,1,2,0:T(8,128)S(1)} collective-permute-done((f32[1,16,16,256]{3,1,2,0:T(8,128)S(1)}, f32[1,16,16,256]{3,1,2,0:T(8,128)S(1)}, u32[]{:S(2)}, u32[]{:S(2)}) %collective-permute-start) | collective-permute-done | bytes 262176 | tf_op jit(solution)/shard_map/while/body/eval_jaxpr/ppermute | solution.py:24
  158.2 10.4 %collective-permute-done = f32[1,16,16,256]{3,1,2,0:T(8,128)S(1)} collective-permute-done((f32[1,16,16,256]{3,1,2,0:T(8,128)S(1)}, f32[1,16,16,256]{3,1,2,0:T(8,128)S(1)}, u32[]{:S(2)}, u32[]{:S(2)}) %collective-permute-start) | collective-permute-done | bytes 262176 | tf_op jit(solution)/shard_map/while/body/eval_jaxpr/ppermute | solution.py:24
  171.0 9.6 %collective-permute-done = f32[1,16,16,256]{3,1,2,0:T(8,128)S(1)} collective-permute-done((f32[1,16,16,256]{3,1,2,0:T(8,128)S(1)}, f32[1,16,16,256]{3,1,2,0:T(8,128)S(1)}, u32[]{:S(2)}, u32[]{:S(2)}) %collective-permute-start) | collective-permute-done | bytes 262176 | tf_op jit(solution)/shard_map/while/body/eval_jaxpr/ppermute | solution.py:24
  183.0 9.3 %collective-permute-done = f32[1,16,16,256]{3,1,2,0:T(8,128)S(1)} collective-permute-done((f32[1,16,16,256]{3,1,2,0:T(8,128)S(1)}, f32[1,16,16,256]{3,1,2,0:T(8,128)S(1)}, u32[]{:S(2)}, u32[]{:S(2)}) %collective-permute-start) | collective-permute-done | bytes 262176 | tf_op jit(solution)/shard_map/while/body/eval_jaxpr/ppermute | solution.py:24
  194.8 9.3 %collective-permute-done = f32[1,16,16,256]{3,1,2,0:T(8,128)S(1)} collective-permute-done((f32[1,16,16,256]{3,1,2,0:T(8,128)S(1)}, f32[1,16,16,256]{3,1,2,0:T(8,128)S(1)}, u32[]{:S(2)}, u32[]{:S(2)}) %collective-permute-start) | collective-permute-done | bytes 262176 | tf_op jit(solution)/shard_map/while/body/eval_jaxpr/ppermute | solution.py:24
  206.5 9.3 %collective-permute-done = f32[1,16,16,256]{3,1,2,0:T(8,128)S(1)} collective-permute-done((f32[1,16,16,256]{3,1,2,0:T(8,128)S(1)}, f32[1,16,16,256]{3,1,2,0:T(8,128)S(1)}, u32[]{:S(2)}, u32[]{:S(2)}) %collective-permute-start) | collective-permute-done | bytes 262176 | tf_op jit(solution)/shard_map/while/body/eval_jaxpr/ppermute | solution.py:24
  215.9 1.9 collective-permute-start
  218.2 9.3 %collective-permute-done = f32[1,16,16,256]{3,1,2,0:T(8,128)S(1)} collective-permute-done((f32[1,16,16,256]{3,1,2,0:T(8,128)S(1)}, f32[1,16,16,256]{3,1,2,0:T(8,128)S(1)}, u32[]{:S(2)}, u32[]{:S(2)}) %collective-permute-start) | collective-permute-done | bytes 262176 | tf_op jit(solution)/shard_map/while/body/eval_jaxpr/ppermute | solution.py:24
  229.9 9.5 %collective-permute-done = f32[1,16,16,256]{3,1,2,0:T(8,128)S(1)} collective-permute-done((f32[1,16,16,256]{3,1,2,0:T(8,128)S(1)}, f32[1,16,16,256]{3,1,2,0:T(8,128)S(1)}, u32[]{:S(2)}, u32[]{:S(2)}) %collective-permute-start) | collective-permute-done | bytes 262176 | tf_op jit(solution)/shard_map/while/body/eval_jaxpr/ppermute | solution.py:24
  241.8 10.6 %collective-permute-done = f32[1,16,16,256]{3,1,2,0:T(8,128)S(1)} collective-permute-done((f32[1,16,16,256]{3,1,2,0:T(8,128)S(1)}, f32[1,16,16,256]{3,1,2,0:T(8,128)S(1)}, u32[]{:S(2)}, u32[]{:S(2)}) %collective-permute-start) | collective-permute-done | bytes 262176 | tf_op jit(solution)/shard_map/while/body/eval_jaxpr/ppermute | solution.py:24
  254.9 11.8 %collective-permute-done = f32[1,16,16,256]{3,1,2,0:T(8,128)S(1)} collective-permute-done((f32[1,16,16,256]{3,1,2,0:T(8,128)S(1)}, f32[1,16,16,256]{3,1,2,0:T(8,128)S(1)}, u32[]{:S(2)}, u32[]{:S(2)}) %collective-permute-start) | collective-permute-done | bytes 262176 | tf_op jit(solution)/shard_map/while/body/eval_jaxpr/ppermute | solution.py:24
  269.1 11.2 %collective-permute-done = f32[1,16,16,256]{3,1,2,0:T(8,128)S(1)} collective-permute-done((f32[1,16,16,256]{3,1,2,0:T(8,128)S(1)}, f32[1,16,16,256]{3,1,2,0:T(8,128)S(1)}, u32[]{:S(2)}, u32[]{:S(2)}) %collective-permute-start) | collective-permute-done | bytes 262176 | tf_op jit(solution)/shard_map/while/body/eval_jaxpr/ppermute | solution.py:24
  282.8 10.4 %collective-permute-done = f32[1,16,16,256]{3,1,2,0:T(8,128)S(1)} collective-permute-done((f32[1,16,16,256]{3,1,2,0:T(8,128)S(1)}, f32[1,16,16,256]{3,1,2,0:T(8,128)S(1)}, u32[]{:S(2)}, u32[]{:S(2)}) %collective-permute-start) | collective-permute-done | bytes 262176 | tf_op jit(solution)/shard_map/while/body/eval_jaxpr/ppermute | solution.py:24
  295.7 9.5 %collective-permute-done = f32[1,16,16,256]{3,1,2,0:T(8,128)S(1)} collective-permute-done((f32[1,16,16,256]{3,1,2,0:T(8,128)S(1)}, f32[1,16,16,256]{3,1,2,0:T(8,128)S(1)}, u32[]{:S(2)}, u32[]{:S(2)}) %collective-permute-start) | collective-permute-done | bytes 262176 | tf_op jit(solution)/shard_map/while/body/eval_jaxpr/ppermute | solution.py:24
  307.6 9.3 %collective-permute-done = f32[1,16,16,256]{3,1,2,0:T(8,128)S(1)} collective-permute-done((f32[1,16,16,256]{3,1,2,0:T(8,128)S(1)}, f32[1,16,16,256]{3,1,2,0:T(8,128)S(1)}, u32[]{:S(2)}, u32[]{:S(2)}) %collective-permute-start) | collective-permute-done | bytes 262176 | tf_op jit(solution)/shard_map/while/body/eval_jaxpr/ppermute | solution.py:24
  319.3 9.3 %collective-permute-done = f32[1,16,16,256]{3,1,2,0:T(8,128)S(1)} collective-permute-done((f32[1,16,16,256]{3,1,2,0:T(8,128)S(1)}, f32[1,16,16,256]{3,1,2,0:T(8,128)S(1)}, u32[]{:S(2)}, u32[]{:S(2)}) %collective-permute-start) | collective-permute-done | bytes 262176 | tf_op jit(solution)/shard_map/while/body/eval_jaxpr/ppermute | solution.py:24
  331.1 10.0 %collective-permute-done = f32[1,16,16,256]{3,1,2,0:T(8,128)S(1)} collective-permute-done((f32[1,16,16,256]{3,1,2,0:T(8,128)S(1)}, f32[1,16,16,256]{3,1,2,0:T(8,128)S(1)}, u32[]{:S(2)}, u32[]{:S(2)}) %collective-permute-start) | collective-permute-done | bytes 262176 | tf_op jit(solution)/shard_map/while/body/eval_jaxpr/ppermute | solution.py:24
  341.2 3.7 conditional.2
  347.3 9.3 %collective-permute-done = f32[1,16,16,256]{3,1,2,0:T(8,128)S(1)} collective-permute-done((f32[1,16,16,256]{3,1,2,0:T(8,128)S(1)}, f32[1,16,16,256]{3,1,2,0:T(8,128)S(1)}, u32[]{:S(2)}, u32[]{:S(2)}) %collective-permute-start) | collective-permute-done | bytes 262176 | tf_op jit(solution)/shard_map/while/body/eval_jaxpr/ppermute | solution.py:24
  356.6 3.7 conditional.2
  362.7 9.3 %collective-permute-done = f32[1,16,16,256]{3,1,2,0:T(8,128)S(1)} collective-permute-done((f32[1,16,16,256]{3,1,2,0:T(8,128)S(1)}, f32[1,16,16,256]{3,1,2,0:T(8,128)S(1)}, u32[]{:S(2)}, u32[]{:S(2)}) %collective-permute-start) | collective-permute-done | bytes 262176 | tf_op jit(solution)/shard_map/while/body/eval_jaxpr/ppermute | solution.py:24
  372.1 2.3 collective-permute-start
  374.8 10.0 %collective-permute-done = f32[1,16,16,256]{3,1,2,0:T(8,128)S(1)} collective-permute-done((f32[1,16,16,256]{3,1,2,0:T(8,128)S(1)}, f32[1,16,16,256]{3,1,2,0:T(8,128)S(1)}, u32[]{:S(2)}, u32[]{:S(2)}) %collective-permute-start) | collective-permute-done | bytes 262176 | tf_op jit(solution)/shard_map/while/body/eval_jaxpr/ppermute | solution.py:24
  387.2 11.5 %collective-permute-done = f32[1,16,16,256]{3,1,2,0:T(8,128)S(1)} collective-permute-done((f32[1,16,16,256]{3,1,2,0:T(8,128)S(1)}, f32[1,16,16,256]{3,1,2,0:T(8,128)S(1)}, u32[]{:S(2)}, u32[]{:S(2)}) %collective-permute-start) | collective-permute-done | bytes 262176 | tf_op jit(solution)/shard_map/while/body/eval_jaxpr/ppermute | solution.py:24
  401.2 11.5 %collective-permute-done = f32[1,16,16,256]{3,1,2,0:T(8,128)S(1)} collective-permute-done((f32[1,16,16,256]{3,1,2,0:T(8,128)S(1)}, f32[1,16,16,256]{3,1,2,0:T(8,128)S(1)}, u32[]{:S(2)}, u32[]{:S(2)}) %collective-permute-start) | collective-permute-done | bytes 262176 | tf_op jit(solution)/shard_map/while/body/eval_jaxpr/ppermute | solution.py:24
  415.1 10.6 %collective-permute-done = f32[1,16,16,256]{3,1,2,0:T(8,128)S(1)} collective-permute-done((f32[1,16,16,256]{3,1,2,0:T(8,128)S(1)}, f32[1,16,16,256]{3,1,2,0:T(8,128)S(1)}, u32[]{:S(2)}, u32[]{:S(2)}) %collective-permute-start) | collective-permute-done | bytes 262176 | tf_op jit(solution)/shard_map/while/body/eval_jaxpr/ppermute | solution.py:24
  428.2 9.8 %collective-permute-done = f32[1,16,16,256]{3,1,2,0:T(8,128)S(1)} collective-permute-done((f32[1,16,16,256]{3,1,2,0:T(8,128)S(1)}, f32[1,16,16,256]{3,1,2,0:T(8,128)S(1)}, u32[]{:S(2)}, u32[]{:S(2)}) %collective-permute-start) | collective-permute-done | bytes 262176 | tf_op jit(solution)/shard_map/while/body/eval_jaxpr/ppermute | solution.py:24
  440.4 9.3 %collective-permute-done = f32[1,16,16,256]{3,1,2,0:T(8,128)S(1)} collective-permute-done((f32[1,16,16,256]{3,1,2,0:T(8,128)S(1)}, f32[1,16,16,256]{3,1,2,0:T(8,128)S(1)}, u32[]{:S(2)}, u32[]{:S(2)}) %collective-permute-start) | collective-permute-done | bytes 262176 | tf_op jit(solution)/shard_map/while/body/eval_jaxpr/ppermute | solution.py:24
  452.1 9.3 %collective-permute-done = f32[1,16,16,256]{3,1,2,0:T(8,128)S(1)} collective-permute-done((f32[1,16,16,256]{3,1,2,0:T(8,128)S(1)}, f32[1,16,16,256]{3,1,2,0:T(8,128)S(1)}, u32[]{:S(2)}, u32[]{:S(2)}) %collective-permute-start) | collective-permute-done | bytes 262176 | tf_op jit(solution)/shard_map/while/body/eval_jaxpr/ppermute | solution.py:24
  463.8 9.3 %collective-permute-done = f32[1,16,16,256]{3,1,2,0:T(8,128)S(1)} collective-permute-done((f32[1,16,16,256]{3,1,2,0:T(8,128)S(1)}, f32[1,16,16,256]{3,1,2,0:T(8,128)S(1)}, u32[]{:S(2)}, u32[]{:S(2)}) %collective-permute-start) | collective-permute-done | bytes 262176 | tf_op jit(solution)/shard_map/while/body/eval_jaxpr/ppermute | solution.py:24
  475.6 9.3 %collective-permute-done = f32[1,16,16,256]{3,1,2,0:T(8,128)S(1)} collective-permute-done((f32[1,16,16,256]{3,1,2,0:T(8,128)S(1)}, f32[1,16,16,256]{3,1,2,0:T(8,128)S(1)}, u32[]{:S(2)}, u32[]{:S(2)}) %collective-permute-start) | collective-permute-done | bytes 262176 | tf_op jit(solution)/shard_map/while/body/eval_jaxpr/ppermute | solution.py:24
  487.3 9.3 %collective-permute-done = f32[1,16,16,256]{3,1,2,0:T(8,128)S(1)} collective-permute-done((f32[1,16,16,256]{3,1,2,0:T(8,128)S(1)}, f32[1,16,16,256]{3,1,2,0:T(8,128)S(1)}, u32[]{:S(2)}, u32[]{:S(2)}) %collective-permute-start) | collective-permute-done | bytes 262176 | tf_op jit(solution)/shard_map/while/body/eval_jaxpr/ppermute | solution.py:24
  499.0 10.4 %collective-permute-done = f32[1,16,16,256]{3,1,2,0:T(8,128)S(1)} collective-permute-done((f32[1,16,16,256]{3,1,2,0:T(8,128)S(1)}, f32[1,16,16,256]{3,1,2,0:T(8,128)S(1)}, u32[]{:S(2)}, u32[]{:S(2)}) %collective-permute-start) | collective-permute-done | bytes 262176 | tf_op jit(solution)/shard_map/while/body/eval_jaxpr/ppermute | solution.py:24
  511.9 11.6 %collective-permute-done = f32[1,16,16,256]{3,1,2,0:T(8,128)S(1)} collective-permute-done((f32[1,16,16,256]{3,1,2,0:T(8,128)S(1)}, f32[1,16,16,256]{3,1,2,0:T(8,128)S(1)}, u32[]{:S(2)}, u32[]{:S(2)}) %collective-permute-start) | collective-permute-done | bytes 262176 | tf_op jit(solution)/shard_map/while/body/eval_jaxpr/ppermute | solution.py:24
  525.9 9.3 %collective-permute-done = f32[1,16,16,256]{3,1,2,0:T(8,128)S(1)} collective-permute-done((f32[1,16,16,256]{3,1,2,0:T(8,128)S(1)}, f32[1,16,16,256]{3,1,2,0:T(8,128)S(1)}, u32[]{:S(2)}, u32[]{:S(2)}) %collective-permute-start) | collective-permute-done | bytes 262176 | tf_op jit(solution)/shard_map/while/body/eval_jaxpr/ppermute | solution.py:24
  537.6 9.3 %collective-permute-done = f32[1,16,16,256]{3,1,2,0:T(8,128)S(1)} collective-permute-done((f32[1,16,16,256]{3,1,2,0:T(8,128)S(1)}, f32[1,16,16,256]{3,1,2,0:T(8,128)S(1)}, u32[]{:S(2)}, u32[]{:S(2)}) %collective-permute-start) | collective-permute-done | bytes 262176 | tf_op jit(solution)/shard_map/while/body/eval_jaxpr/ppermute | solution.py:24
  549.3 9.3 %collective-permute-done = f32[1,16,16,256]{3,1,2,0:T(8,128)S(1)} collective-permute-done((f32[1,16,16,256]{3,1,2,0:T(8,128)S(1)}, f32[1,16,16,256]{3,1,2,0:T(8,128)S(1)}, u32[]{:S(2)}, u32[]{:S(2)}) %collective-permute-start) | collective-permute-done | bytes 262176 | tf_op jit(solution)/shard_map/while/body/eval_jaxpr/ppermute | solution.py:24
  (317 shorter events, 96.1 us)
Async XLA Ops:
  0.0 15.3 %copy-start = (f32[1,2,16,16,256]{4,3,2,1,0:T(8,128)S(1)}, f32[1,2,16,16,256]{4,3,2,1,0:T(8,128)}, u32[]{:S(2)}) copy-start(f32[1,2,16,16,256]{4,3,2,1,0:T(8,128)} %param.8) | copy-start | bytes 1572868
  15.6 0.7 copy-start.2
  64.0 19.2 %collective-permute-start.1 = (f32[2,16,16,256]{3,1,2,0:T(8,128)S(1)}, f32[2,16,16,256]{3,1,2,0:T(8,128)S(1)}, u32[]{:S(2)}, u32[]{:S(2)}) collective-permute-start(f32[2,16,16,256]{3,1,2,0:T(8,128)S(1)} %fusion.78), channel_id=1, source_target_pairs={{0,8},{8,16},{16,24},{24,32},{32,40},{40,48},{48,56},{56,64},{64,7... | collective-permute-start | bytes 1572872 | tf_op jit(solution)/shard_map/ppermute | solution.py:24
  142.1 13.6 %collective-permute-start = (f32[1,16,16,256]{3,1,2,0:T(8,128)S(1)}, f32[1,16,16,256]{3,1,2,0:T(8,128)S(1)}, u32[]{:S(2)}, u32[]{:S(2)}) collective-permute-start(f32[1,16,16,256]{3,1,2,0:T(8,128)S(1)} %get-tuple-element.503), channel_id=1, source_target_pairs={{0,8},{8,16},{16,24},{24,32},{32,40},{40,48},{48,56},{56,64},{64,7... | collective-permute-start | bytes 786440 | tf_op jit(solution)/shard_map/while/body/eval_jaxpr/ppermute | solution.py:24
  155.8 12.7 %collective-permute-start = (f32[1,16,16,256]{3,1,2,0:T(8,128)S(1)}, f32[1,16,16,256]{3,1,2,0:T(8,128)S(1)}, u32[]{:S(2)}, u32[]{:S(2)}) collective-permute-start(f32[1,16,16,256]{3,1,2,0:T(8,128)S(1)} %get-tuple-element.503), channel_id=1, source_target_pairs={{0,8},{8,16},{16,24},{24,32},{32,40},{40,48},{48,56},{56,64},{64,7... | collective-permute-start | bytes 786440 | tf_op jit(solution)/shard_map/while/body/eval_jaxpr/ppermute | solution.py:24
  168.7 11.9 %collective-permute-start = (f32[1,16,16,256]{3,1,2,0:T(8,128)S(1)}, f32[1,16,16,256]{3,1,2,0:T(8,128)S(1)}, u32[]{:S(2)}, u32[]{:S(2)}) collective-permute-start(f32[1,16,16,256]{3,1,2,0:T(8,128)S(1)} %get-tuple-element.503), channel_id=1, source_target_pairs={{0,8},{8,16},{16,24},{24,32},{32,40},{40,48},{48,56},{56,64},{64,7... | collective-permute-start | bytes 786440 | tf_op jit(solution)/shard_map/while/body/eval_jaxpr/ppermute | solution.py:24
  180.7 11.6 %collective-permute-start = (f32[1,16,16,256]{3,1,2,0:T(8,128)S(1)}, f32[1,16,16,256]{3,1,2,0:T(8,128)S(1)}, u32[]{:S(2)}, u32[]{:S(2)}) collective-permute-start(f32[1,16,16,256]{3,1,2,0:T(8,128)S(1)} %get-tuple-element.503), channel_id=1, source_target_pairs={{0,8},{8,16},{16,24},{24,32},{32,40},{40,48},{48,56},{56,64},{64,7... | collective-permute-start | bytes 786440 | tf_op jit(solution)/shard_map/while/body/eval_jaxpr/ppermute | solution.py:24
  192.4 11.6 %collective-permute-start = (f32[1,16,16,256]{3,1,2,0:T(8,128)S(1)}, f32[1,16,16,256]{3,1,2,0:T(8,128)S(1)}, u32[]{:S(2)}, u32[]{:S(2)}) collective-permute-start(f32[1,16,16,256]{3,1,2,0:T(8,128)S(1)} %get-tuple-element.503), channel_id=1, source_target_pairs={{0,8},{8,16},{16,24},{24,32},{32,40},{40,48},{48,56},{56,64},{64,7... | collective-permute-start | bytes 786440 | tf_op jit(solution)/shard_map/while/body/eval_jaxpr/ppermute | solution.py:24
  204.2 11.6 %collective-permute-start = (f32[1,16,16,256]{3,1,2,0:T(8,128)S(1)}, f32[1,16,16,256]{3,1,2,0:T(8,128)S(1)}, u32[]{:S(2)}, u32[]{:S(2)}) collective-permute-start(f32[1,16,16,256]{3,1,2,0:T(8,128)S(1)} %get-tuple-element.503), channel_id=1, source_target_pairs={{0,8},{8,16},{16,24},{24,32},{32,40},{40,48},{48,56},{56,64},{64,7... | collective-permute-start | bytes 786440 | tf_op jit(solution)/shard_map/while/body/eval_jaxpr/ppermute | solution.py:24
  215.9 11.6 %collective-permute-start = (f32[1,16,16,256]{3,1,2,0:T(8,128)S(1)}, f32[1,16,16,256]{3,1,2,0:T(8,128)S(1)}, u32[]{:S(2)}, u32[]{:S(2)}) collective-permute-start(f32[1,16,16,256]{3,1,2,0:T(8,128)S(1)} %get-tuple-element.503), channel_id=1, source_target_pairs={{0,8},{8,16},{16,24},{24,32},{32,40},{40,48},{48,56},{56,64},{64,7... | collective-permute-start | bytes 786440 | tf_op jit(solution)/shard_map/while/body/eval_jaxpr/ppermute | solution.py:24
  227.6 11.8 %collective-permute-start = (f32[1,16,16,256]{3,1,2,0:T(8,128)S(1)}, f32[1,16,16,256]{3,1,2,0:T(8,128)S(1)}, u32[]{:S(2)}, u32[]{:S(2)}) collective-permute-start(f32[1,16,16,256]{3,1,2,0:T(8,128)S(1)} %get-tuple-element.503), channel_id=1, source_target_pairs={{0,8},{8,16},{16,24},{24,32},{32,40},{40,48},{48,56},{56,64},{64,7... | collective-permute-start | bytes 786440 | tf_op jit(solution)/shard_map/while/body/eval_jaxpr/ppermute | solution.py:24
  239.5 12.9 %collective-permute-start = (f32[1,16,16,256]{3,1,2,0:T(8,128)S(1)}, f32[1,16,16,256]{3,1,2,0:T(8,128)S(1)}, u32[]{:S(2)}, u32[]{:S(2)}) collective-permute-start(f32[1,16,16,256]{3,1,2,0:T(8,128)S(1)} %get-tuple-element.503), channel_id=1, source_target_pairs={{0,8},{8,16},{16,24},{24,32},{32,40},{40,48},{48,56},{56,64},{64,7... | collective-permute-start | bytes 786440 | tf_op jit(solution)/shard_map/while/body/eval_jaxpr/ppermute | solution.py:24
  252.6 14.1 %collective-permute-start = (f32[1,16,16,256]{3,1,2,0:T(8,128)S(1)}, f32[1,16,16,256]{3,1,2,0:T(8,128)S(1)}, u32[]{:S(2)}, u32[]{:S(2)}) collective-permute-start(f32[1,16,16,256]{3,1,2,0:T(8,128)S(1)} %get-tuple-element.503), channel_id=1, source_target_pairs={{0,8},{8,16},{16,24},{24,32},{32,40},{40,48},{48,56},{56,64},{64,7... | collective-permute-start | bytes 786440 | tf_op jit(solution)/shard_map/while/body/eval_jaxpr/ppermute | solution.py:24
  266.8 13.6 %collective-permute-start = (f32[1,16,16,256]{3,1,2,0:T(8,128)S(1)}, f32[1,16,16,256]{3,1,2,0:T(8,128)S(1)}, u32[]{:S(2)}, u32[]{:S(2)}) collective-permute-start(f32[1,16,16,256]{3,1,2,0:T(8,128)S(1)} %get-tuple-element.503), channel_id=1, source_target_pairs={{0,8},{8,16},{16,24},{24,32},{32,40},{40,48},{48,56},{56,64},{64,7... | collective-permute-start | bytes 786440 | tf_op jit(solution)/shard_map/while/body/eval_jaxpr/ppermute | solution.py:24
  280.5 12.7 %collective-permute-start = (f32[1,16,16,256]{3,1,2,0:T(8,128)S(1)}, f32[1,16,16,256]{3,1,2,0:T(8,128)S(1)}, u32[]{:S(2)}, u32[]{:S(2)}) collective-permute-start(f32[1,16,16,256]{3,1,2,0:T(8,128)S(1)} %get-tuple-element.503), channel_id=1, source_target_pairs={{0,8},{8,16},{16,24},{24,32},{32,40},{40,48},{48,56},{56,64},{64,7... | collective-permute-start | bytes 786440 | tf_op jit(solution)/shard_map/while/body/eval_jaxpr/ppermute | solution.py:24
  293.3 11.8 %collective-permute-start = (f32[1,16,16,256]{3,1,2,0:T(8,128)S(1)}, f32[1,16,16,256]{3,1,2,0:T(8,128)S(1)}, u32[]{:S(2)}, u32[]{:S(2)}) collective-permute-start(f32[1,16,16,256]{3,1,2,0:T(8,128)S(1)} %get-tuple-element.503), channel_id=1, source_target_pairs={{0,8},{8,16},{16,24},{24,32},{32,40},{40,48},{48,56},{56,64},{64,7... | collective-permute-start | bytes 786440 | tf_op jit(solution)/shard_map/while/body/eval_jaxpr/ppermute | solution.py:24
  305.3 11.6 %collective-permute-start = (f32[1,16,16,256]{3,1,2,0:T(8,128)S(1)}, f32[1,16,16,256]{3,1,2,0:T(8,128)S(1)}, u32[]{:S(2)}, u32[]{:S(2)}) collective-permute-start(f32[1,16,16,256]{3,1,2,0:T(8,128)S(1)} %get-tuple-element.503), channel_id=1, source_target_pairs={{0,8},{8,16},{16,24},{24,32},{32,40},{40,48},{48,56},{56,64},{64,7... | collective-permute-start | bytes 786440 | tf_op jit(solution)/shard_map/while/body/eval_jaxpr/ppermute | solution.py:24
  317.0 11.6 %collective-permute-start = (f32[1,16,16,256]{3,1,2,0:T(8,128)S(1)}, f32[1,16,16,256]{3,1,2,0:T(8,128)S(1)}, u32[]{:S(2)}, u32[]{:S(2)}) collective-permute-start(f32[1,16,16,256]{3,1,2,0:T(8,128)S(1)} %get-tuple-element.503), channel_id=1, source_target_pairs={{0,8},{8,16},{16,24},{24,32},{32,40},{40,48},{48,56},{56,64},{64,7... | collective-permute-start | bytes 786440 | tf_op jit(solution)/shard_map/while/body/eval_jaxpr/ppermute | solution.py:24
  328.7 12.4 %collective-permute-start = (f32[1,16,16,256]{3,1,2,0:T(8,128)S(1)}, f32[1,16,16,256]{3,1,2,0:T(8,128)S(1)}, u32[]{:S(2)}, u32[]{:S(2)}) collective-permute-start(f32[1,16,16,256]{3,1,2,0:T(8,128)S(1)} %get-tuple-element.503), channel_id=1, source_target_pairs={{0,8},{8,16},{16,24},{24,32},{32,40},{40,48},{48,56},{56,64},{64,7... | collective-permute-start | bytes 786440 | tf_op jit(solution)/shard_map/while/body/eval_jaxpr/ppermute | solution.py:24
  341.2 1.6 copy-start.3
  344.9 11.6 %collective-permute-start = (f32[1,16,16,256]{3,1,2,0:T(8,128)S(1)}, f32[1,16,16,256]{3,1,2,0:T(8,128)S(1)}, u32[]{:S(2)}, u32[]{:S(2)}) collective-permute-start(f32[1,16,16,256]{3,1,2,0:T(8,128)S(1)} %get-tuple-element.503), channel_id=1, source_target_pairs={{0,8},{8,16},{16,24},{24,32},{32,40},{40,48},{48,56},{56,64},{64,7... | collective-permute-start | bytes 786440 | tf_op jit(solution)/shard_map/while/body/eval_jaxpr/ppermute | solution.py:24
  356.6 1.6 copy-start.3
  360.3 11.6 %collective-permute-start = (f32[1,16,16,256]{3,1,2,0:T(8,128)S(1)}, f32[1,16,16,256]{3,1,2,0:T(8,128)S(1)}, u32[]{:S(2)}, u32[]{:S(2)}) collective-permute-start(f32[1,16,16,256]{3,1,2,0:T(8,128)S(1)} %get-tuple-element.503), channel_id=1, source_target_pairs={{0,8},{8,16},{16,24},{24,32},{32,40},{40,48},{48,56},{56,64},{64,7... | collective-permute-start | bytes 786440 | tf_op jit(solution)/shard_map/while/body/eval_jaxpr/ppermute | solution.py:24
  372.1 12.7 %collective-permute-start = (f32[1,16,16,256]{3,1,2,0:T(8,128)S(1)}, f32[1,16,16,256]{3,1,2,0:T(8,128)S(1)}, u32[]{:S(2)}, u32[]{:S(2)}) collective-permute-start(f32[1,16,16,256]{3,1,2,0:T(8,128)S(1)} %get-tuple-element.503), channel_id=1, source_target_pairs={{0,8},{8,16},{16,24},{24,32},{32,40},{40,48},{48,56},{56,64},{64,7... | collective-permute-start | bytes 786440 | tf_op jit(solution)/shard_map/while/body/eval_jaxpr/ppermute | solution.py:24
  384.9 13.8 %collective-permute-start = (f32[1,16,16,256]{3,1,2,0:T(8,128)S(1)}, f32[1,16,16,256]{3,1,2,0:T(8,128)S(1)}, u32[]{:S(2)}, u32[]{:S(2)}) collective-permute-start(f32[1,16,16,256]{3,1,2,0:T(8,128)S(1)} %get-tuple-element.503), channel_id=1, source_target_pairs={{0,8},{8,16},{16,24},{24,32},{32,40},{40,48},{48,56},{56,64},{64,7... | collective-permute-start | bytes 786440 | tf_op jit(solution)/shard_map/while/body/eval_jaxpr/ppermute | solution.py:24
  398.9 13.8 %collective-permute-start = (f32[1,16,16,256]{3,1,2,0:T(8,128)S(1)}, f32[1,16,16,256]{3,1,2,0:T(8,128)S(1)}, u32[]{:S(2)}, u32[]{:S(2)}) collective-permute-start(f32[1,16,16,256]{3,1,2,0:T(8,128)S(1)} %get-tuple-element.503), channel_id=1, source_target_pairs={{0,8},{8,16},{16,24},{24,32},{32,40},{40,48},{48,56},{56,64},{64,7... | collective-permute-start | bytes 786440 | tf_op jit(solution)/shard_map/while/body/eval_jaxpr/ppermute | solution.py:24
  412.8 12.9 %collective-permute-start = (f32[1,16,16,256]{3,1,2,0:T(8,128)S(1)}, f32[1,16,16,256]{3,1,2,0:T(8,128)S(1)}, u32[]{:S(2)}, u32[]{:S(2)}) collective-permute-start(f32[1,16,16,256]{3,1,2,0:T(8,128)S(1)} %get-tuple-element.503), channel_id=1, source_target_pairs={{0,8},{8,16},{16,24},{24,32},{32,40},{40,48},{48,56},{56,64},{64,7... | collective-permute-start | bytes 786440 | tf_op jit(solution)/shard_map/while/body/eval_jaxpr/ppermute | solution.py:24
  425.9 12.1 %collective-permute-start = (f32[1,16,16,256]{3,1,2,0:T(8,128)S(1)}, f32[1,16,16,256]{3,1,2,0:T(8,128)S(1)}, u32[]{:S(2)}, u32[]{:S(2)}) collective-permute-start(f32[1,16,16,256]{3,1,2,0:T(8,128)S(1)} %get-tuple-element.503), channel_id=1, source_target_pairs={{0,8},{8,16},{16,24},{24,32},{32,40},{40,48},{48,56},{56,64},{64,7... | collective-permute-start | bytes 786440 | tf_op jit(solution)/shard_map/while/body/eval_jaxpr/ppermute | solution.py:24
  438.1 11.6 %collective-permute-start = (f32[1,16,16,256]{3,1,2,0:T(8,128)S(1)}, f32[1,16,16,256]{3,1,2,0:T(8,128)S(1)}, u32[]{:S(2)}, u32[]{:S(2)}) collective-permute-start(f32[1,16,16,256]{3,1,2,0:T(8,128)S(1)} %get-tuple-element.503), channel_id=1, source_target_pairs={{0,8},{8,16},{16,24},{24,32},{32,40},{40,48},{48,56},{56,64},{64,7... | collective-permute-start | bytes 786440 | tf_op jit(solution)/shard_map/while/body/eval_jaxpr/ppermute | solution.py:24
  449.8 11.6 %collective-permute-start = (f32[1,16,16,256]{3,1,2,0:T(8,128)S(1)}, f32[1,16,16,256]{3,1,2,0:T(8,128)S(1)}, u32[]{:S(2)}, u32[]{:S(2)}) collective-permute-start(f32[1,16,16,256]{3,1,2,0:T(8,128)S(1)} %get-tuple-element.503), channel_id=1, source_target_pairs={{0,8},{8,16},{16,24},{24,32},{32,40},{40,48},{48,56},{56,64},{64,7... | collective-permute-start | bytes 786440 | tf_op jit(solution)/shard_map/while/body/eval_jaxpr/ppermute | solution.py:24
  461.5 11.6 %collective-permute-start = (f32[1,16,16,256]{3,1,2,0:T(8,128)S(1)}, f32[1,16,16,256]{3,1,2,0:T(8,128)S(1)}, u32[]{:S(2)}, u32[]{:S(2)}) collective-permute-start(f32[1,16,16,256]{3,1,2,0:T(8,128)S(1)} %get-tuple-element.503), channel_id=1, source_target_pairs={{0,8},{8,16},{16,24},{24,32},{32,40},{40,48},{48,56},{56,64},{64,7... | collective-permute-start | bytes 786440 | tf_op jit(solution)/shard_map/while/body/eval_jaxpr/ppermute | solution.py:24
  473.2 11.6 %collective-permute-start = (f32[1,16,16,256]{3,1,2,0:T(8,128)S(1)}, f32[1,16,16,256]{3,1,2,0:T(8,128)S(1)}, u32[]{:S(2)}, u32[]{:S(2)}) collective-permute-start(f32[1,16,16,256]{3,1,2,0:T(8,128)S(1)} %get-tuple-element.503), channel_id=1, source_target_pairs={{0,8},{8,16},{16,24},{24,32},{32,40},{40,48},{48,56},{56,64},{64,7... | collective-permute-start | bytes 786440 | tf_op jit(solution)/shard_map/while/body/eval_jaxpr/ppermute | solution.py:24
  484.9 11.6 %collective-permute-start = (f32[1,16,16,256]{3,1,2,0:T(8,128)S(1)}, f32[1,16,16,256]{3,1,2,0:T(8,128)S(1)}, u32[]{:S(2)}, u32[]{:S(2)}) collective-permute-start(f32[1,16,16,256]{3,1,2,0:T(8,128)S(1)} %get-tuple-element.503), channel_id=1, source_target_pairs={{0,8},{8,16},{16,24},{24,32},{32,40},{40,48},{48,56},{56,64},{64,7... | collective-permute-start | bytes 786440 | tf_op jit(solution)/shard_map/while/body/eval_jaxpr/ppermute | solution.py:24
  496.7 12.7 %collective-permute-start = (f32[1,16,16,256]{3,1,2,0:T(8,128)S(1)}, f32[1,16,16,256]{3,1,2,0:T(8,128)S(1)}, u32[]{:S(2)}, u32[]{:S(2)}) collective-permute-start(f32[1,16,16,256]{3,1,2,0:T(8,128)S(1)} %get-tuple-element.503), channel_id=1, source_target_pairs={{0,8},{8,16},{16,24},{24,32},{32,40},{40,48},{48,56},{56,64},{64,7... | collective-permute-start | bytes 786440 | tf_op jit(solution)/shard_map/while/body/eval_jaxpr/ppermute | solution.py:24
  509.5 13.9 %collective-permute-start = (f32[1,16,16,256]{3,1,2,0:T(8,128)S(1)}, f32[1,16,16,256]{3,1,2,0:T(8,128)S(1)}, u32[]{:S(2)}, u32[]{:S(2)}) collective-permute-start(f32[1,16,16,256]{3,1,2,0:T(8,128)S(1)} %get-tuple-element.503), channel_id=1, source_target_pairs={{0,8},{8,16},{16,24},{24,32},{32,40},{40,48},{48,56},{56,64},{64,7... | collective-permute-start | bytes 786440 | tf_op jit(solution)/shard_map/while/body/eval_jaxpr/ppermute | solution.py:24
  523.5 11.6 %collective-permute-start = (f32[1,16,16,256]{3,1,2,0:T(8,128)S(1)}, f32[1,16,16,256]{3,1,2,0:T(8,128)S(1)}, u32[]{:S(2)}, u32[]{:S(2)}) collective-permute-start(f32[1,16,16,256]{3,1,2,0:T(8,128)S(1)} %get-tuple-element.503), channel_id=1, source_target_pairs={{0,8},{8,16},{16,24},{24,32},{32,40},{40,48},{48,56},{56,64},{64,7... | collective-permute-start | bytes 786440 | tf_op jit(solution)/shard_map/while/body/eval_jaxpr/ppermute | solution.py:24
  535.3 11.6 %collective-permute-start = (f32[1,16,16,256]{3,1,2,0:T(8,128)S(1)}, f32[1,16,16,256]{3,1,2,0:T(8,128)S(1)}, u32[]{:S(2)}, u32[]{:S(2)}) collective-permute-start(f32[1,16,16,256]{3,1,2,0:T(8,128)S(1)} %get-tuple-element.503), channel_id=1, source_target_pairs={{0,8},{8,16},{16,24},{24,32},{32,40},{40,48},{48,56},{56,64},{64,7... | collective-permute-start | bytes 786440 | tf_op jit(solution)/shard_map/while/body/eval_jaxpr/ppermute | solution.py:24
  547.0 11.6 %collective-permute-start = (f32[1,16,16,256]{3,1,2,0:T(8,128)S(1)}, f32[1,16,16,256]{3,1,2,0:T(8,128)S(1)}, u32[]{:S(2)}, u32[]{:S(2)}) collective-permute-start(f32[1,16,16,256]{3,1,2,0:T(8,128)S(1)} %get-tuple-element.503), channel_id=1, source_target_pairs={{0,8},{8,16},{16,24},{24,32},{32,40},{40,48},{48,56},{56,64},{64,7... | collective-permute-start | bytes 786440 | tf_op jit(solution)/shard_map/while/body/eval_jaxpr/ppermute | solution.py:24
  558.6 0.8 copy-start.1
where the time goes:
time: 561 us; the launch traced here: 559 us
  waiting for transfers between devices  343 us (61%)
  blocking collectives  91 us (16%)
  starting transfers between devices  67.2 us (12%)
  matrix products  22.6 us (4%)
  local copies, waits for them, and re-layouts  18.2 us (3%)
  other arithmetic  13.4 us (2%)
    ppermute x34, waiting for transfers between devices, passed_along(): return lax.ppermute(block, axis, route)  343 us
    psum x16, blocking collectives, by_axis(): return functools.reduce(lax.psum, axes, shard)  91 us
    ppermute x34, starting transfers between devices, passed_along(): return lax.ppermute(block, axis, route)  67.2 us
    conv_general_dilated x10, matrix products, convolve(): lax.conv_general_dilated(activated, kernel, (1, 1), 'SAME', dimension_num...  22.6 us
  transfers between devices with their start and end apart: 34, of which 34 were waited for; matrix products, arithmetic and copies ran while one was open for 2% of the time, Pallas kernels for 0%

commit v1 on v0

v1 whole, which is shorter than its diff:
```python
import functools

import jax
import jax.numpy as jnp
from jax import lax
from jax.experimental import pallas as pl
from jax.experimental.pallas import tpu as pltpu
from jax.sharding import Mesh
from jax.sharding import PartitionSpec as P

MESH = pl.DeviceIdType.MESH
FINE = 0.125
COARSE = 0.5
EPSILON = 1e-05
LAYERS = 4
COLUMN = 4
SAMPLES = 2
EXCHANGES = 8
EARLY = 5


def remote(src, dst, send_sem, recv_sem, device):
    return pltpu.make_async_remote_copy(
        src_ref=src,
        dst_ref=dst,
        send_sem=send_sem,
        recv_sem=recv_sem,
        device_id=device,
        device_id_type=MESH,
    )


def kernel(
    planes,
    chips,
    iterate,
    weights,
    gains,
    offsets,
    out,
    kept,
    state,
    begin,
    kernels,
    padded,
    sums,
    passed_sums,
    forcing,
    chain,
    wide,
    coarse,
    params,
    local_sem,
    sums_send,
    sums_recv,
    pass_send,
    pass_recv,
    wide_send,
    wide_recv,
    force_send,
    force_recv,
    param_send,
    param_recv,
    start_send,
    chain_send,
    chain_recv,
    out_send,
    out_recv,
):
    side, channels = iterate.shape[1], iterate.shape[3]
    rows = side * side
    z, y, x, core = (lax.axis_index(name) for name in ("z", "y", "x", "core"))
    peers = chips * 2
    me = x * 2 + core
    entries = float(peers * SAMPLES * rows)
    position = z * COLUMN + y
    up, down = lax.rem(y + 1, COLUMN), lax.rem(y + COLUMN - 1, COLUMN)
    above, below = lax.rem(z + 1, planes), lax.rem(z + planes - 1, planes)
    next_z = jnp.where(y == COLUMN - 1, above, z)

    for layer in range(LAYERS):
        pltpu.make_async_copy(weights.at[layer], kernels.at[layer], local_sem.at[layer]).start()

    barrier = pltpu.get_barrier_semaphore()
    greeted = 0
    for step in range(1, peers):
        other = lax.rem(me + step, peers)
        pl.semaphore_signal(
            barrier,
            inc=1,
            device_id={"x": other // 2, "core": lax.rem(other, 2)},
            device_id_type=MESH,
        )
        greeted += 1
    for step in range(1, COLUMN):
        for half in range(2):
            pl.semaphore_signal(
                barrier,
                inc=1,
                device_id={"y": lax.rem(y + step, COLUMN), "core": half},
                device_id_type=MESH,
            )
            greeted += 1
    for plane, row in ((above, y), (below, y), (above, up), (below, down)):
        pl.semaphore_signal(
            barrier, inc=1, device_id={"z": plane, "y": row}, device_id_type=MESH
        )
        greeted += 1

    def peer_copy(exchange, step, sender_step):
        other = lax.rem(me + step, peers)
        sender = lax.rem(me + sender_step, peers)
        return remote(
            sums.at[exchange, me],
            sums.at[exchange, me],
            sums_send.at[exchange, step],
            sums_recv.at[exchange, sender],
            {"x": other // 2, "core": lax.rem(other, 2)},
        )

    def send_sums(exchange):
        for step in range(1, peers):
            peer_copy(exchange, step, 0).start()

    def gather_sums(exchange):
        for step in range(1, peers):
            peer_copy(exchange, step, step).wait_recv()
        total = sums[exchange, 0]
        for peer in range(1, peers):
            total = total + sums[exchange, peer]
        return total

    def statistics(total):
        center = total[0:1] / entries
        inverse = lax.rsqrt(total[1:2] / entries - center * center + EPSILON)
        return center, inverse

    place = lax.broadcasted_iota(jnp.int32, (side, channels), 0)

    def activate(source, count, center, gain, offset):
        for sample in range(count):
            for row in range(side):
                value = jnp.maximum((source[sample, row] - center) * gain + offset, 0.0)
                left = jnp.where(place == 0, 0.0, pltpu.roll(value, 1, axis=0))
                right = jnp.where(place == side - 1, 0.0, pltpu.roll(value, side - 1, axis=0))
                padded[sample, row + 1, :, 0:channels] = left.astype(jnp.bfloat16)
                padded[sample, row + 1, :, channels : 2 * channels] = value.astype(jnp.bfloat16)
                padded[sample, row + 1, :, 2 * channels :] = right.astype(jnp.bfloat16)

    def convolve(sample, kernel_at):
        total = None
        for tap in range(3):
            taken = padded[sample, tap : tap + side].reshape(rows, 3 * channels)
            product = jnp.dot(taken, kernel_at(tap), preferred_element_type=jnp.float32)
            total = product if total is None else total + product
        return total.reshape(side, side, channels)

    def folded(value):
        return jnp.sum(value.reshape(rows // 8, 8, channels), axis=0)

    def store_sums(exchange, plain, square):
        sums[exchange, me] = jnp.concatenate(
            [jnp.sum(plain, axis=0, keepdims=True), jnp.sum(square, axis=0, keepdims=True)], axis=0
        )

    edge = jnp.zeros((side, 3 * channels), jnp.bfloat16)
    for sample in range(SAMPLES):
        padded[sample, 0] = edge
        padded[sample, side + 1] = edge

    plain = square = jnp.zeros((8, channels), jnp.float32)
    for sample in range(SAMPLES):
        value = iterate[sample]
        state[sample] = value
        plain, square = plain + folded(value), square + folded(value * value)
    store_sums(0, plain, square)
    pl.semaphore_wait(barrier, greeted)
    send_sums(0)

    def start_copy(sample):
        return remote(
            iterate.at[sample],
            chain.at[0],
            start_send.at[sample],
            chain_recv.at[0],
            {"y": 2 * core + sample, "core": 1},
        )

    @pl.when(position == 0)
    def _():
        for sample in range(SAMPLES):
            start_copy(sample).start()

    def wide_copy(way, tap, slot):
        target = (up, down, up, down)[way]
        return remote(
            wide.at[slot, tap],
            wide.at[slot, tap],
            wide_send.at[way, tap],
            wide_recv.at[way, tap],
            {"y": target, "core": 1},
        )

    rightward = tuple(range(9))
    leftward = tuple(range(8, -1, -1))

    for layer in range(1):
        pltpu.make_async_copy(weights.at[layer], kernels.at[layer], local_sem.at[layer]).wait()

    @pl.when(core == 1)
    def _():
        for tap in range(9):
            wide[y, tap] = kernels[
                0, tap // 3, (tap % 3) * channels : (tap % 3 + 1) * channels
            ].astype(jnp.float32)
        for count in range(EARLY):
            wide_copy(0, rightward[count], y).start()
            wide_copy(1, leftward[count], y).start()
        pltpu.make_async_copy(weights.at[0], coarse.at[y], local_sem.at[LAYERS]).start()

    def relax(layer, carry):
        center, inverse = statistics(gather_sums(layer))
        activate(state, SAMPLES, center, gains[layer] * inverse, offsets[layer])

        @pl.when(layer > 0)
        def _():
            pltpu.make_async_copy(weights.at[layer], kernels.at[layer], local_sem.at[layer]).wait()

        plain = square = jnp.zeros((8, channels), jnp.float32)
        for sample in range(SAMPLES):
            value = state[sample] + FINE * convolve(sample, lambda tap: kernels[layer, tap])
            state[sample] = value
            plain, square = plain + folded(value), square + folded(value * value)
        store_sums(layer + 1, plain, square)
        send_sums(layer + 1)
        return carry

    lax.fori_loop(0, LAYERS, relax, 0)

    following = {"z": next_z, "y": up}
    relaxed_copy = remote(state, begin, pass_send.at[0], pass_recv.at[0], following)
    relaxed_copy.start()

    @pl.when(core == 1)
    def _():
        for count in range(EARLY, 9):
            wide_copy(0, rightward[count], y).start()
            wide_copy(1, leftward[count], y).start()

    passed_sums[0] = gather_sums(LAYERS)
    totals_copy = remote(
        passed_sums.at[0], passed_sums.at[1], pass_send.at[1], pass_recv.at[1], following
    )
    totals_copy.start()
    totals_copy.wait_recv()
    relaxed_copy.wait_recv()

    @pl.when(position == 0)
    def _():
        first = sums[0, 0]
        for peer in range(1, peers):
            first = first + sums[0, peer]
        passed_sums[1] = first
        for sample in range(SAMPLES):
            begin[sample] = iterate[sample]

    center, inverse = statistics(passed_sums[1])
    gain, offset = gains[0] * inverse, offsets[0]
    params[y, 0:1] = center
    params[y, 1:2] = gain
    params[y, 2:3] = offset

    def param_copy(step, sender_step):
        return remote(
            params.at[y],
            params.at[y],
            param_send.at[step],
            param_recv.at[lax.rem(y + sender_step, COLUMN)],
            {"y": lax.rem(y + step, COLUMN), "core": 1},
        )

    @pl.when(core == 1)
    def _():
        for step in range(1, COLUMN):
            param_copy(step, 0).start()

    activate(begin, SAMPLES, center, gain, offset)
    relaxed_copy.wait_send()
    plain = square = jnp.zeros((8, channels), jnp.float32)
    for sample in range(SAMPLES):
        increment = convolve(sample, lambda tap: kernels[0, tap])
        value = begin[sample]
        kept[sample] = value + COARSE * increment
        value = value + FINE * increment
        state[sample] = value
        plain, square = plain + folded(value), square + folded(value * value)
    store_sums(LAYERS + 1, plain, square)
    send_sums(LAYERS + 1)

    @pl.when(core == 1)
    def _():
        for count in range(EARLY):
            tap = rightward[count]
            wide_copy(0, tap, down).wait_recv()
            wide_copy(2, tap, down).start()
        for count in range(9 - EARLY):
            tap = leftward[count]
            wide_copy(1, tap, up).wait_recv()
            wide_copy(3, tap, up).start()

    def refine(layer, carry):
        center, inverse = statistics(gather_sums(LAYERS + layer))
        activate(state, SAMPLES, center, gains[layer] * inverse, offsets[layer])
        plain = square = jnp.zeros((8, channels), jnp.float32)
        for sample in range(SAMPLES):
            value = state[sample] + FINE * convolve(sample, lambda tap: kernels[layer, tap])
            state[sample] = value
            plain, square = plain + folded(value), square + folded(value * value)
        store_sums(LAYERS + layer + 1, plain, square)
        send_sums(LAYERS + layer + 1)
        return carry

    lax.fori_loop(1, LAYERS - 1, refine, 0)

    def force_copy(sample):
        return remote(
            kept.at[sample],
            forcing.at[y],
            force_send.at[sample],
            force_recv.at[y],
            {"y": 2 * core + sample, "core": 1},
        )

    last = LAYERS - 1
    center, inverse = statistics(gather_sums(LAYERS + last))
    activate(state, SAMPLES, center, gains[last] * inverse, offsets[last])
    for sample in range(SAMPLES):
        value = state[sample] + FINE * convolve(sample, lambda tap: kernels[last, tap])
        value = value - kept[sample]
        kept[sample] = value
        here = (core == 1) & (y == 2 * core + sample)

        @pl.when(here)
        def _():
            forcing[y] = kept[sample]

        @pl.when(jnp.logical_not(here))
        def _():
            force_copy(sample).start()

    holder = y // 2
    slot = lax.rem(y, 2)

    def out_copy(block):
        return remote(
            chain.at[block + 1],
            out.at[slot],
            out_send.at[block],
            out_recv.at[slot],
            {"y": block, "core": holder},
        )

    hop = remote(
        chain.at[COLUMN], chain.at[0], chain_send.at[0], chain_recv.at[0], {"z": above, "core": 1}
    )

    @pl.when(core == 1)
    def _():
        for count in range(EARLY, 9):
            wide_copy(0, rightward[count], down).wait_recv()
            wide_copy(1, leftward[count], up).wait_recv()
        for count in range(9 - EARLY, EARLY):
            wide_copy(1, leftward[count], up).wait_recv()
        for count in range(EARLY):
            wide_copy(2, rightward[count], 0).wait_recv()
        for count in range(9 - EARLY):
            wide_copy(3, leftward[count], 0).wait_recv()
        for step in range(1, COLUMN):
            origin = lax.rem(y + step, COLUMN)
            for tap in range(9):
                coarse[
                    origin, tap // 3, (tap % 3) * channels : (tap % 3 + 1) * channels
                ] = wide[origin, tap].astype(jnp.bfloat16)
            param_copy(step, step).wait_recv()
        pltpu.make_async_copy(weights.at[0], coarse.at[y], local_sem.at[LAYERS]).wait()
        for block in range(COLUMN):

            @pl.when(jnp.logical_or(block != y, y < 2))
            def _():
                remote(
                    kept.at[0],
                    forcing.at[block],
                    force_send.at[0],
                    force_recv.at[block],
                    {"y": block, "core": 1},
                ).wait_recv()

        hop.wait_recv()
        for block in range(COLUMN):
            activate(
                chain.at[pl.ds(block, 1)],
                1,
                params[block, 0:1],
                params[block, 1:2],
                params[block, 2:3],
            )
            increment = convolve(0, lambda tap: coarse[block, tap])
            chain[block + 1] = chain[block] + COARSE * increment + forcing[block]
            here = (y == block) & (holder == 1)

            @pl.when(here)
            def _():
                out[slot] = chain[block + 1]

            @pl.when(jnp.logical_not(here))
            def _():
                out_copy(block).start()

        @pl.when(z < planes - 1)
        def _():
            hop.start()

    for sample in range(SAMPLES):

        @pl.when(jnp.logical_not((core == 1) & (y == 2 + sample)))
        def _():
            remote(
                chain.at[1],
                out.at[sample],
                out_send.at[0],
                out_recv.at[sample],
                {"y": y, "core": core},
            ).wait_recv()

    for exchange in range(EXCHANGES):
        for step in range(1, peers):
            peer_copy(exchange, step, 0).wait_send()
    totals_copy.wait_send()
    for sample in range(SAMPLES):

        @pl.when(position == 0)
        def _():
            start_copy(sample).wait_send()

        @pl.when(jnp.logical_not((core == 1) & (y == 2 * core + sample)))
        def _():
            force_copy(sample).wait_send()

    @pl.when(core == 1)
    def _():
        for tap in range(9):
            wide_copy(0, tap, y).wait_send()
            wide_copy(1, tap, y).wait_send()
        for count in range(EARLY):
            wide_copy(2, rightward[count], down).wait_send()
        for count in range(9 - EARLY):
            wide_copy(3, leftward[count], up).wait_send()
        for step in range(1, COLUMN):
            param_copy(step, 0).wait_send()
        for block in range(COLUMN):

            @pl.when(jnp.logical_not((y == block) & (holder == 1)))
            def _():
                out_copy(block).wait_send()

        @pl.when(z < planes - 1)
        def _():
            hop.wait_send()


def block_solve(planes, chips, iterate, weights, gains, offsets):
    _, samples, side, _, channels = iterate.shape
    state = (samples, side, side, channels)
    peers = chips * 2
    dma = pltpu.SemaphoreType.DMA
    result = pl.pallas_call(
        functools.partial(kernel, planes, chips),
        out_shape=jax.ShapeDtypeStruct(state, jnp.float32),
        in_specs=[
            pl.BlockSpec(memory_space=pltpu.VMEM),
            pl.BlockSpec(memory_space=pl.ANY),
            pl.BlockSpec(memory_space=pltpu.VMEM),
            pl.BlockSpec(memory_space=pltpu.VMEM),
        ],
        out_specs=pl.BlockSpec(memory_space=pltpu.VMEM),
        scratch_shapes=[
            pltpu.VMEM(state, jnp.float32),
            pltpu.VMEM(state, jnp.float32),
            pltpu.VMEM(state, jnp.float32),
            pltpu.VMEM((LAYERS, 3, 3 * channels, channels), jnp.bfloat16),
            pltpu.VMEM((samples, side + 2, side, 3 * channels), jnp.bfloat16),
            pltpu.VMEM((EXCHANGES, peers, 2, channels), jnp.float32),
            pltpu.VMEM((2, 2, channels), jnp.float32),
            pltpu.VMEM((COLUMN, side, side, channels), jnp.float32),
            pltpu.VMEM((COLUMN + 1, side, side, channels), jnp.float32),
            pltpu.VMEM((COLUMN, 9, channels, channels), jnp.float32),
            pltpu.VMEM((COLUMN, 3, 3 * channels, channels), jnp.bfloat16),
            pltpu.VMEM((COLUMN, 8, channels), jnp.float32),
            dma((LAYERS + 1,)),
            dma((EXCHANGES, peers)),
            dma((EXCHANGES, peers)),
            dma((2,)),
            dma((2,)),
            dma((4, 9)),
            dma((4, 9)),
            dma((samples,)),
            dma((COLUMN,)),
            dma((COLUMN,)),
            dma((COLUMN,)),
            dma((samples,)),
            dma((1,)),
            dma((1,)),
            dma((COLUMN,)),
            dma((samples,)),
        ],
        compiler_params=pltpu.CompilerParams(
            collective_id=0, has_side_effects=True, vmem_limit_bytes=60 << 20
        ),
    )(
        iterate[0],
        weights.reshape(LAYERS, 3, 3 * channels, channels),
        gains.reshape(LAYERS, 1, channels),
        offsets.reshape(LAYERS, 1, channels),
    )
    return result[None]


def solution(mesh):
    planes = mesh.shape["depth"] // COLUMN
    chips = mesh.shape["batch"] // 2
    finer = Mesh(
        mesh.devices.reshape(planes, COLUMN, chips, 2), ("z", "y", "x", "core")
    )
    depth, batch = ("z", "y"), ("x", "core")
    return jax.shard_map(
        functools.partial(block_solve, planes, chips),
        mesh=finer,
        in_specs=(
            P(depth, batch, None, None, None),
            P(depth, None, None, None, None),
            P(depth, None),
            P(depth, None),
        ),
        out_specs=P(depth, batch, None, None, None),
        check_vma=False,
    )
```

time: 561 us -> 142 us (0.25)
  the two profiles are of different devices: /device:TPU:130 before, /device:TPU:229 now
where the time goes in v1:
time: 142 us; the launch traced here: 140 us
  Pallas kernels  136 us (96%)
  local copies, waits for them, and re-layouts  4.43 us (3%)
    pallas_call x1, Pallas kernels, block_solve(): pl.pallas_call(functools.partial(kernel, planes, chips), out_shape=jax.Sh...  136 us

profile of v1, /device:TPU:229, one launch (start us, length us, event | category | flops | bytes accessed | tf_op | source)
XLA Modules:
  0.0 140.4 jit_solution(16249401059041282033)
XLA Ops:
  0.0 1.3 reshape.10.gains
  1.3 1.3 reshape.11.offsets
  2.6 135.9 %shard_map.46 = f32[2,16,16,256]{3,2,1,0:T(8,128)} custom-call(f32[2,16,16,256]{3,2,1,0:T(8,128)} %bitcast.5, bf16[4,3,768,256]{3,2,1,0:T(8,128)(2,1)} %bitcast.3, f32[4,1,256]{2,1,0:T(1,128)} %reshape.10.gains, f32[4,1,256]{2,1,0:T(1,128)} %reshape.11.offsets), custom_call_target="tpu_custom_call" | custom-call | tf_op jit(solution)/shard_map/pallas_call | solution.py:476
  138.5 1.9 %copy.6 = f32[1,2,16,16,256]{4,3,2,1,0:T(8,128)} copy(f32[1,2,16,16,256]{4,3,2,1,0:T(8,128)} %bitcast.4) | data formatting | bytes 1048576

commit v2 on v1

--- a/solution.py
+++ b/solution.py
@@ -16,7 +16,9 @@
 COLUMN = 4
 SAMPLES = 2
 EXCHANGES = 8
-EARLY = 5
+EARLY = 7
+RELAYED = 5
+HALVES = 2
 
 
 def remote(src, dst, send_sem, recv_sem, device):
@@ -75,37 +77,43 @@
     entries = float(peers * SAMPLES * rows)
     position = z * COLUMN + y
     up, down = lax.rem(y + 1, COLUMN), lax.rem(y + COLUMN - 1, COLUMN)
-    above, below = lax.rem(z + 1, planes), lax.rem(z + planes - 1, planes)
+    above = lax.rem(z + 1, planes)
     next_z = jnp.where(y == COLUMN - 1, above, z)
 
     for layer in range(LAYERS):
         pltpu.make_async_copy(weights.at[layer], kernels.at[layer], local_sem.at[layer]).start()
 
     barrier = pltpu.get_barrier_semaphore()
-    greeted = 0
+
+    def greet(device):
+        pl.semaphore_signal(barrier, inc=1, device_id=device, device_id_type=MESH)
+
     for step in range(1, peers):
         other = lax.rem(me + step, peers)
-        pl.semaphore_signal(
-            barrier,
-            inc=1,
-            device_id={"x": other // 2, "core": lax.rem(other, 2)},
-            device_id_type=MESH,
-        )
-        greeted += 1
+        greet({"x": other // 2, "core": lax.rem(other, 2)})
     for step in range(1, COLUMN):
-        for half in range(2):
-            pl.semaphore_signal(
-                barrier,
-                inc=1,
-                device_id={"y": lax.rem(y + step, COLUMN), "core": half},
-                device_id_type=MESH,
-            )
-            greeted += 1
-    for plane, row in ((above, y), (below, y), (above, up), (below, down)):
-        pl.semaphore_signal(
-            barrier, inc=1, device_id={"z": plane, "y": row}, device_id_type=MESH
-        )
-        greeted += 1
+        greet({"y": lax.rem(y + step, COLUMN), "core": 1})
+
+    @pl.when(core == 1)
+    def _():
+        for step in range(1, COLUMN):
+            greet({"y": lax.rem(y + step, COLUMN), "core": 0})
+
+    @pl.when(position > 0)
+    def _():
+        greet({"z": jnp.where(y == 0, z - 1, z), "y": down})
+
+    @pl.when((core == 1) & (z > 0))
+    def _():
+        greet({"z": z - 1})
+
+    final = planes * COLUMN - 1
+    greeted = (
+        peers - 1
+        + (COLUMN - 1) * (1 + core)
+        + jnp.where(position < final, 1, 0)
+        + jnp.where(z < planes - 1, core, 0)
+    )
 
     def peer_copy(exchange, step, sender_step):
         other = lax.rem(me + step, peers)
@@ -137,9 +145,9 @@
 
     place = lax.broadcasted_iota(jnp.int32, (side, channels), 0)
 
-    def activate(source, count, center, gain, offset):
+    def activate(source, count, center, gain, offset, taken=range(side)):
         for sample in range(count):
-            for row in range(side):
+            for row in taken:
                 value = jnp.maximum((source[sample, row] - center) * gain + offset, 0.0)
                 left = jnp.where(place == 0, 0.0, pltpu.roll(value, 1, axis=0))
                 right = jnp.where(place == side - 1, 0.0, pltpu.roll(value, side - 1, axis=0))
@@ -147,13 +155,14 @@
                 padded[sample, row + 1, :, channels : 2 * channels] = value.astype(jnp.bfloat16)
                 padded[sample, row + 1, :, 2 * channels :] = right.astype(jnp.bfloat16)
 
-    def convolve(sample, kernel_at):
+    def convolve(sample, kernel_at, first=0, count=side):
         total = None
         for tap in range(3):
-            taken = padded[sample, tap : tap + side].reshape(rows, 3 * channels)
+            taken = padded[sample, first + tap : first + tap + count]
+            taken = taken.reshape(count * side, 3 * channels)
             product = jnp.dot(taken, kernel_at(tap), preferred_element_type=jnp.float32)
             total = product if total is None else total + product
-        return total.reshape(side, side, channels)
+        return total.reshape(count, side, channels)
 
     def folded(value):
         return jnp.sum(value.reshape(rows // 8, 8, channels), axis=0)
@@ -177,19 +186,22 @@
     pl.semaphore_wait(barrier, greeted)
     send_sums(0)
 
-    def start_copy(sample):
-        return remote(
-            iterate.at[sample],
-            chain.at[0],
-            start_send.at[sample],
-            chain_recv.at[0],
+    half = side // HALVES
+
+    def start_copy(sample, part):
+        return remote(
+            iterate.at[sample, pl.ds(part * half, half)],
+            chain.at[0, pl.ds(part * half, half)],
+            start_send.at[sample, part],
+            chain_recv.at[part],
             {"y": 2 * core + sample, "core": 1},
         )
 
     @pl.when(position == 0)
     def _():
         for sample in range(SAMPLES):
-            start_copy(sample).start()
+            for part in range(HALVES):
+                start_copy(sample, part).start()
 
     def wide_copy(way, tap, slot):
         target = (up, down, up, down)[way]
@@ -220,7 +232,7 @@
 
     def relax(layer, carry):
         center, inverse = statistics(gather_sums(layer))
-        activate(state, SAMPLES, center, gains[layer] * inverse, offsets[layer])
+        activate(state, SAMPLES, center, gains[pl.ds(layer, 1)] * inverse, offsets[pl.ds(layer, 1)])
 
         @pl.when(layer > 0)
         def _():
@@ -239,7 +251,10 @@
 
     following = {"z": next_z, "y": up}
     relaxed_copy = remote(state, begin, pass_send.at[0], pass_recv.at[0], following)
-    relaxed_copy.start()
+
+    @pl.when(position < final)
+    def _():
+        relaxed_copy.start()
 
     @pl.when(core == 1)
     def _():
@@ -251,9 +266,15 @@
     totals_copy = remote(
         passed_sums.at[0], passed_sums.at[1], pass_send.at[1], pass_recv.at[1], following
     )
-    totals_copy.start()
-    totals_copy.wait_recv()
-    relaxed_copy.wait_recv()
+
+    @pl.when(position < final)
+    def _():
+        totals_copy.start()
+
+    @pl.when(position > 0)
+    def _():
+        totals_copy.wait_recv()
+        relaxed_copy.wait_recv()
 
     @pl.when(position == 0)
     def _():
@@ -265,7 +286,7 @@
             begin[sample] = iterate[sample]
 
     center, inverse = statistics(passed_sums[1])
-    gain, offset = gains[0] * inverse, offsets[0]
+    gain, offset = gains[0:1] * inverse, offsets[0:1]
     params[y, 0:1] = center
     params[y, 1:2] = gain
     params[y, 2:3] = offset
@@ -285,7 +306,11 @@
             param_copy(step, 0).start()
 
     activate(begin, SAMPLES, center, gain, offset)
-    relaxed_copy.wait_send()
+
+    @pl.when(position < final)
+    def _():
+        relaxed_copy.wait_send()
+
     plain = square = jnp.zeros((8, channels), jnp.float32)
     for sample in range(SAMPLES):
         increment = convolve(sample, lambda tap: kernels[0, tap])
@@ -299,18 +324,18 @@
 
     @pl.when(core == 1)
     def _():
-        for count in range(EARLY):
+        for count in range(RELAYED):
             tap = rightward[count]
             wide_copy(0, tap, down).wait_recv()
             wide_copy(2, tap, down).start()
-        for count in range(9 - EARLY):
-            tap = leftward[count]
-            wide_copy(1, tap, up).wait_recv()
-            wide_copy(3, tap, up).start()
+            if count < 9 - RELAYED:
+                tap = leftward[count]
+                wide_copy(1, tap, up).wait_recv()
+                wide_copy(3, tap, up).start()
 
     def refine(layer, carry):
         center, inverse = statistics(gather_sums(LAYERS + layer))
-        activate(state, SAMPLES, center, gains[layer] * inverse, offsets[layer])
+        activate(state, SAMPLES, center, gains[pl.ds(layer, 1)] * inverse, offsets[pl.ds(layer, 1)])
         plain = square = jnp.zeros((8, channels), jnp.float32)
         for sample in range(SAMPLES):
             value = state[sample] + FINE * convolve(sample, lambda tap: kernels[layer, tap])
@@ -333,7 +358,7 @@
 
     last = LAYERS - 1
     center, inverse = statistics(gather_sums(LAYERS + last))
-    activate(state, SAMPLES, center, gains[last] * inverse, offsets[last])
+    activate(state, SAMPLES, center, gains[last : last + 1] * inverse, offsets[last : last + 1])
     for sample in range(SAMPLES):
         value = state[sample] + FINE * convolve(sample, lambda tap: kernels[last, tap])
         value = value - kept[sample]
@@ -360,20 +385,27 @@
             {"y": block, "core": holder},
         )
 
-    hop = remote(
-        chain.at[COLUMN], chain.at[0], chain_send.at[0], chain_recv.at[0], {"z": above, "core": 1}
-    )
-
-    @pl.when(core == 1)
-    def _():
-        for count in range(EARLY, 9):
+    def hop(part):
+        return remote(
+            chain.at[COLUMN, pl.ds(part * half, half)],
+            chain.at[0, pl.ds(part * half, half)],
+            chain_send.at[part],
+            chain_recv.at[part],
+            {"z": above, "core": 1},
+        )
+
+    def own_copy(block):
+        return pltpu.make_async_copy(chain.at[block + 1], out.at[slot], local_sem.at[LAYERS + 1])
+
+    @pl.when(core == 1)
+    def _():
+        for count in range(RELAYED, 9):
             wide_copy(0, rightward[count], down).wait_recv()
+        for count in range(9 - RELAYED, 9):
             wide_copy(1, leftward[count], up).wait_recv()
-        for count in range(9 - EARLY, EARLY):
-            wide_copy(1, leftward[count], up).wait_recv()
-        for count in range(EARLY):
+        for count in range(RELAYED):
             wide_copy(2, rightward[count], 0).wait_recv()
-        for count in range(9 - EARLY):
+        for count in range(9 - RELAYED):
             wide_copy(3, leftward[count], 0).wait_recv()
         for step in range(1, COLUMN):
             origin = lax.rem(y + step, COLUMN)
@@ -384,6 +416,14 @@
             param_copy(step, step).wait_recv()
         pltpu.make_async_copy(weights.at[0], coarse.at[y], local_sem.at[LAYERS]).wait()
         for block in range(COLUMN):
+            center, gain, offset = (params[block, row : row + 1] for row in range(3))
+            source = chain.at[pl.ds(block, 1)]
+            if block == 0:
+                for part in range(HALVES):
+                    hop(part).wait_recv()
+                    activate(source, 1, center, gain, offset, range(part * half, part * half + half))
+            else:
+                activate(source, 1, center, gain, offset)
 
             @pl.when(jnp.logical_or(block != y, y < 2))
             def _():
@@ -395,30 +435,35 @@
                     {"y": block, "core": 1},
                 ).wait_recv()
 
-        hop.wait_recv()
-        for block in range(COLUMN):
-            activate(
-                chain.at[pl.ds(block, 1)],
-                1,
-                params[block, 0:1],
-                params[block, 1:2],
-                params[block, 2:3],
-            )
-            increment = convolve(0, lambda tap: coarse[block, tap])
-            chain[block + 1] = chain[block] + COARSE * increment + forcing[block]
+            if block < COLUMN - 1:
+                increment = convolve(0, lambda tap: coarse[block, tap])
+                chain[block + 1] = chain[block] + COARSE * increment + forcing[block]
+            else:
+                for part in range(HALVES):
+                    first = part * half
+                    taken = pl.ds(first, half)
+                    increment = convolve(0, lambda tap: coarse[block, tap], first, half)
+                    chain[block + 1, taken] = (
+                        chain[block, taken] + COARSE * increment + forcing[block, taken]
+                    )
+
+                    @pl.when(z < planes - 1)
+                    def _():
+                        hop(part).start()
+
             here = (y == block) & (holder == 1)
 
             @pl.when(here)
             def _():
-                out[slot] = chain[block + 1]
+                own_copy(block).start()
 
             @pl.when(jnp.logical_not(here))
             def _():
                 out_copy(block).start()
 
-        @pl.when(z < planes - 1)
-        def _():
-            hop.start()
+        @pl.when(holder == 1)
+        def _():
+            own_copy(0).wait()
 
     for sample in range(SAMPLES):
 
@@ -435,12 +480,17 @@
     for exchange in range(EXCHANGES):
         for step in range(1, peers):
             peer_copy(exchange, step, 0).wait_send()
-    totals_copy.wait_send()
+
+    @pl.when(position < final)
+    def _():
+        totals_copy.wait_send()
+
     for sample in range(SAMPLES):
 
         @pl.when(position == 0)
         def _():
-            start_copy(sample).wait_send()
+            for part in range(HALVES):
+                start_copy(sample, part).wait_send()
 
         @pl.when(jnp.logical_not((core == 1) & (y == 2 * core + sample)))
         def _():
@@ -451,9 +501,9 @@
         for tap in range(9):
             wide_copy(0, tap, y).wait_send()
             wide_copy(1, tap, y).wait_send()
-        for count in range(EARLY):
+        for count in range(RELAYED):
             wide_copy(2, rightward[count], down).wait_send()
-        for count in range(9 - EARLY):
+        for count in range(9 - RELAYED):
             wide_copy(3, leftward[count], up).wait_send()
         for step in range(1, COLUMN):
             param_copy(step, 0).wait_send()
@@ -465,7 +515,8 @@
 
         @pl.when(z < planes - 1)
         def _():
-            hop.wait_send()
+            for part in range(HALVES):
+                hop(part).wait_send()
 
 
 def block_solve(planes, chips, iterate, weights, gains, offsets):
@@ -482,7 +533,7 @@
             pl.BlockSpec(memory_space=pltpu.VMEM),
             pl.BlockSpec(memory_space=pltpu.VMEM),
         ],
-        out_specs=pl.BlockSpec(memory_space=pltpu.VMEM),
+        out_specs=pl.BlockSpec(memory_space=pl.ANY),
         scratch_shapes=[
             pltpu.VMEM(state, jnp.float32),
             pltpu.VMEM(state, jnp.float32),
@@ -496,7 +547,7 @@
             pltpu.VMEM((COLUMN, 9, channels, channels), jnp.float32),
             pltpu.VMEM((COLUMN, 3, 3 * channels, channels), jnp.bfloat16),
             pltpu.VMEM((COLUMN, 8, channels), jnp.float32),
-            dma((LAYERS + 1,)),
+            dma((LAYERS + 2,)),
             dma((EXCHANGES, peers)),
             dma((EXCHANGES, peers)),
             dma((2,)),
@@ -507,9 +558,9 @@
             dma((COLUMN,)),
             dma((COLUMN,)),
             dma((COLUMN,)),
-            dma((samples,)),
-            dma((1,)),
-            dma((1,)),
+            dma((samples, HALVES)),
+            dma((HALVES,)),
+            dma((HALVES,)),
             dma((COLUMN,)),
             dma((samples,)),
         ],
@@ -519,8 +570,8 @@
     )(
         iterate[0],
         weights.reshape(LAYERS, 3, 3 * channels, channels),
-        gains.reshape(LAYERS, 1, channels),
-        offsets.reshape(LAYERS, 1, channels),
+        gains,
+        offsets,
     )
     return result[None]
 

time: 142 us -> 133 us (0.937)
  Pallas kernels: 136 us -> 129 us
  local copies, waits for them, and re-layouts: 4.43 us -> 1.87 us
    pallas_call x1, Pallas kernels: 136 us -> 129 us  [block_solve(): pl.pallas_call(functools.partial(kernel, planes, chips), out_shape=jax.Sh...]
    reshape x2 -> x0, local copies, waits for them, and re-layouts: 2.56 us -> none  [the longest x1 1.28 us: block_solve(): gains.reshape(LAYERS, 1, channels)]
where the time goes in v2:
time: 133 us; the launch traced here: 131 us
  Pallas kernels  129 us (97%)
  local copies, waits for them, and re-layouts  1.87 us (1%)
    pallas_call x1, Pallas kernels, block_solve(): pl.pallas_call(functools.partial(kernel, planes, chips), out_shape=jax.Sh...  129 us

profile of v2, /device:TPU:229, one launch (start us, length us, event | category | flops | bytes accessed | tf_op | source)
XLA Modules:
  0.0 131.2 jit_solution(16967690242297282894)
XLA Ops:
  0.0 129.3 %shard_map.46 = f32[2,16,16,256]{3,2,1,0:T(8,128)} custom-call(f32[2,16,16,256]{3,2,1,0:T(8,128)} %bitcast.5, bf16[4,3,768,256]{3,2,1,0:T(8,128)(2,1)} %bitcast.3, f32[4,256]{1,0:T(4,128)} %gains.1, f32[4,256]{1,0:T(4,128)} %offsets.1), custom_call_target="tpu_custom_call" | custom-call | tf_op jit(solution)/shard_map/pallas_call | solution.py:527
  129.3 1.9 %copy.6 = f32[1,2,16,16,256]{4,3,2,1,0:T(8,128)} copy(f32[1,2,16,16,256]{4,3,2,1,0:T(8,128)} %bitcast.4) | data formatting | bytes 1048576

commit v3 on v2

--- a/solution.py
+++ b/solution.py
@@ -16,8 +16,8 @@
 COLUMN = 4
 SAMPLES = 2
 EXCHANGES = 8
-EARLY = 7
-RELAYED = 5
+DIRECT = 5
+SHARED = 4
 HALVES = 2
 
 
@@ -203,18 +203,25 @@
             for part in range(HALVES):
                 start_copy(sample, part).start()
 
-    def wide_copy(way, tap, slot):
-        target = (up, down, up, down)[way]
+    odd = lax.rem(x, 2) == 1
+
+    def wide_copy(way, count, slot):
+        flipped = jnp.logical_not(odd) if way % 2 else odd
+        tap = jnp.where(flipped, 8 - count, count)
+        if way < 4:
+            device = {"y": down if way % 2 else up, "core": 1}
+        else:
+            device = {"x": jnp.where(odd, x - 1, x + 1), "core": 1}
         return remote(
             wide.at[slot, tap],
             wide.at[slot, tap],
-            wide_send.at[way, tap],
-            wide_recv.at[way, tap],
-            {"y": target, "core": 1},
-        )
-
-    rightward = tuple(range(9))
-    leftward = tuple(range(8, -1, -1))
+            wide_send.at[way, count],
+            wide_recv.at[way, count],
+            device,
+        )
+
+    def pair_copy(way, count):
+        return wide_copy(4 + way, count, up if way else down)
 
     for layer in range(1):
         pltpu.make_async_copy(weights.at[layer], kernels.at[layer], local_sem.at[layer]).wait()
@@ -225,9 +232,9 @@
             wide[y, tap] = kernels[
                 0, tap // 3, (tap % 3) * channels : (tap % 3 + 1) * channels
             ].astype(jnp.float32)
-        for count in range(EARLY):
-            wide_copy(0, rightward[count], y).start()
-            wide_copy(1, leftward[count], y).start()
+        for count in range(DIRECT):
+            wide_copy(0, count, y).start()
+            wide_copy(1, count, y).start()
         pltpu.make_async_copy(weights.at[0], coarse.at[y], local_sem.at[LAYERS]).start()
 
     def relax(layer, carry):
@@ -245,6 +252,13 @@
             plain, square = plain + folded(value), square + folded(value * value)
         store_sums(layer + 1, plain, square)
         send_sums(layer + 1)
+        for way in range(2):
+
+            @pl.when((core == 1) & (layer == 1 + way))
+            def _():
+                wide_copy(way, 0, y).wait_recv()
+                pair_copy(way, 0).start()
+
         return carry
 
     lax.fori_loop(0, LAYERS, relax, 0)
@@ -258,9 +272,15 @@
 
     @pl.when(core == 1)
     def _():
-        for count in range(EARLY, 9):
-            wide_copy(0, rightward[count], y).start()
-            wide_copy(1, leftward[count], y).start()
+        for count in range(1, DIRECT):
+            for way in range(2):
+                wide_copy(way, count, y).wait_recv()
+                if count < SHARED - 1:
+                    pair_copy(way, count).start()
+        for count in range(DIRECT):
+            wide_copy(2, count, down).start()
+            if count < 9 - DIRECT:
+                wide_copy(3, count, up).start()
 
     passed_sums[0] = gather_sums(LAYERS)
     totals_copy = remote(
@@ -324,14 +344,7 @@
 
     @pl.when(core == 1)
     def _():
-        for count in range(RELAYED):
-            tap = rightward[count]
-            wide_copy(0, tap, down).wait_recv()
-            wide_copy(2, tap, down).start()
-            if count < 9 - RELAYED:
-                tap = leftward[count]
-                wide_copy(1, tap, up).wait_recv()
-                wide_copy(3, tap, up).start()
+        pair_copy(0, SHARED - 1).start()
 
     def refine(layer, carry):
         center, inverse = statistics(gather_sums(LAYERS + layer))
@@ -343,6 +356,11 @@
             plain, square = plain + folded(value), square + folded(value * value)
         store_sums(LAYERS + layer + 1, plain, square)
         send_sums(LAYERS + layer + 1)
+
+        @pl.when((core == 1) & (layer == 1))
+        def _():
+            pair_copy(1, SHARED - 1).start()
+
         return carry
 
     lax.fori_loop(1, LAYERS - 1, refine, 0)
@@ -399,14 +417,13 @@
 
     @pl.when(core == 1)
     def _():
-        for count in range(RELAYED, 9):
-            wide_copy(0, rightward[count], down).wait_recv()
-        for count in range(9 - RELAYED, 9):
-            wide_copy(1, leftward[count], up).wait_recv()
-        for count in range(RELAYED):
-            wide_copy(2, rightward[count], 0).wait_recv()
-        for count in range(9 - RELAYED):
-            wide_copy(3, leftward[count], 0).wait_recv()
+        for count in range(DIRECT):
+            wide_copy(2, count, 0).wait_recv()
+        for count in range(9 - DIRECT):
+            wide_copy(3, count, 0).wait_recv()
+        for count in range(SHARED):
+            pair_copy(0, count).wait_recv()
+            pair_copy(1, count).wait_recv()
         for step in range(1, COLUMN):
             origin = lax.rem(y + step, COLUMN)
             for tap in range(9):
@@ -498,13 +515,15 @@
 
     @pl.when(core == 1)
     def _():
-        for tap in range(9):
-            wide_copy(0, tap, y).wait_send()
-            wide_copy(1, tap, y).wait_send()
-        for count in range(RELAYED):
-            wide_copy(2, rightward[count], down).wait_send()
-        for count in range(9 - RELAYED):
-            wide_copy(3, leftward[count], up).wait_send()
+        for count in range(DIRECT):
+            wide_copy(0, count, y).wait_send()
+            wide_copy(1, count, y).wait_send()
+            wide_copy(2, count, down).wait_send()
+        for count in range(9 - DIRECT):
+            wide_copy(3, count, up).wait_send()
+        for count in range(SHARED):
+            pair_copy(0, count).wait_send()
+            pair_copy(1, count).wait_send()
         for step in range(1, COLUMN):
             param_copy(step, 0).wait_send()
         for block in range(COLUMN):
@@ -552,8 +571,8 @@
             dma((EXCHANGES, peers)),
             dma((2,)),
             dma((2,)),
-            dma((4, 9)),
-            dma((4, 9)),
+            dma((6, DIRECT)),
+            dma((6, DIRECT)),
             dma((samples,)),
             dma((COLUMN,)),
             dma((COLUMN,)),

time: 133 us -> 137 us (1.030)
  Pallas kernels: 129 us -> 133 us
    pallas_call x1, Pallas kernels: 129 us -> 133 us  [block_solve(): pl.pallas_call(functools.partial(kernel, planes, chips), out_shape=jax.Sh...]
where the time goes in v3:
time: 137 us; the launch traced here: 135 us
  Pallas kernels  133 us (97%)
  local copies, waits for them, and re-layouts  1.87 us (1%)
    pallas_call x1, Pallas kernels, block_solve(): pl.pallas_call(functools.partial(kernel, planes, chips), out_shape=jax.Sh...  133 us

profile of v3, /device:TPU:229, one launch (start us, length us, event | category | flops | bytes accessed | tf_op | source)
XLA Modules:
  0.0 135.4 jit_solution(2315616174179952065)
XLA Ops:
  0.0 133.5 %shard_map.46 = f32[2,16,16,256]{3,2,1,0:T(8,128)} custom-call(f32[2,16,16,256]{3,2,1,0:T(8,128)} %bitcast.5, bf16[4,3,768,256]{3,2,1,0:T(8,128)(2,1)} %bitcast.3, f32[4,256]{1,0:T(4,128)} %gains.1, f32[4,256]{1,0:T(4,128)} %offsets.1), custom_call_target="tpu_custom_call" | custom-call | tf_op jit(solution)/shard_map/pallas_call | solution.py:546
  133.5 1.9 %copy.6 = f32[1,2,16,16,256]{4,3,2,1,0:T(8,128)} copy(f32[1,2,16,16,256]{4,3,2,1,0:T(8,128)} %bitcast.4) | data formatting | bytes 1048576

commit v4 on v3

--- a/solution.py
+++ b/solution.py
@@ -16,9 +16,10 @@
 COLUMN = 4
 SAMPLES = 2
 EXCHANGES = 8
-DIRECT = 5
-SHARED = 4
-HALVES = 2
+DIRECT_RUNS = ((0, 2), (2, 5))
+UP_RUN, DOWN_RUN = (0, 5), (0, 4)
+PAIR_RUNS = ((0, 2), (2, 3), (3, 4))
+HALVES = 1
 
 
 def remote(src, dst, send_sem, recv_sem, device):
@@ -205,23 +206,23 @@
 
     odd = lax.rem(x, 2) == 1
 
-    def wide_copy(way, count, slot):
+    def wide_copy(way, run, slot):
         flipped = jnp.logical_not(odd) if way % 2 else odd
-        tap = jnp.where(flipped, 8 - count, count)
+        taps = pl.ds(jnp.where(flipped, 9 - run[1], run[0]), run[1] - run[0])
         if way < 4:
             device = {"y": down if way % 2 else up, "core": 1}
         else:
             device = {"x": jnp.where(odd, x - 1, x + 1), "core": 1}
         return remote(
-            wide.at[slot, tap],
-            wide.at[slot, tap],
-            wide_send.at[way, count],
-            wide_recv.at[way, count],
+            wide.at[slot, taps],
+            wide.at[slot, taps],
+            wide_send.at[way, run[0]],
+            wide_recv.at[way, run[0]],
             device,
         )
 
-    def pair_copy(way, count):
-        return wide_copy(4 + way, count, up if way else down)
+    def pair_copy(way, run):
+        return wide_copy(4 + way, run, up if way else down)
 
     for layer in range(1):
         pltpu.make_async_copy(weights.at[layer], kernels.at[layer], local_sem.at[layer]).wait()
@@ -232,9 +233,9 @@
             wide[y, tap] = kernels[
                 0, tap // 3, (tap % 3) * channels : (tap % 3 + 1) * channels
             ].astype(jnp.float32)
-        for count in range(DIRECT):
-            wide_copy(0, count, y).start()
-            wide_copy(1, count, y).start()
+        for run in DIRECT_RUNS:
+            wide_copy(0, run, y).start()
+            wide_copy(1, run, y).start()
         pltpu.make_async_copy(weights.at[0], coarse.at[y], local_sem.at[LAYERS]).start()
 
     def relax(layer, carry):
@@ -252,13 +253,6 @@
             plain, square = plain + folded(value), square + folded(value * value)
         store_sums(layer + 1, plain, square)
         send_sums(layer + 1)
-        for way in range(2):
-
-            @pl.when((core == 1) & (layer == 1 + way))
-            def _():
-                wide_copy(way, 0, y).wait_recv()
-                pair_copy(way, 0).start()
-
         return carry
 
     lax.fori_loop(0, LAYERS, relax, 0)
@@ -272,15 +266,13 @@
 
     @pl.when(core == 1)
     def _():
-        for count in range(1, DIRECT):
+        for run in DIRECT_RUNS:
             for way in range(2):
-                wide_copy(way, count, y).wait_recv()
-                if count < SHARED - 1:
-                    pair_copy(way, count).start()
-        for count in range(DIRECT):
-            wide_copy(2, count, down).start()
-            if count < 9 - DIRECT:
-                wide_copy(3, count, up).start()
+                wide_copy(way, run, y).wait_recv()
+        wide_copy(2, UP_RUN, down).start()
+        wide_copy(3, DOWN_RUN, up).start()
+        for way in range(2):
+            pair_copy(way, PAIR_RUNS[0]).start()
 
     passed_sums[0] = gather_sums(LAYERS)
     totals_copy = remote(
@@ -344,7 +336,7 @@
 
     @pl.when(core == 1)
     def _():
-        pair_copy(0, SHARED - 1).start()
+        pair_copy(0, PAIR_RUNS[1]).start()
 
     def refine(layer, carry):
         center, inverse = statistics(gather_sums(LAYERS + layer))
@@ -359,7 +351,12 @@
 
         @pl.when((core == 1) & (layer == 1))
         def _():
-            pair_copy(1, SHARED - 1).start()
+            pair_copy(1, PAIR_RUNS[1]).start()
+
+        @pl.when((core == 1) & (layer == 2))
+        def _():
+            for way in range(2):
+                pair_copy(way, PAIR_RUNS[2]).start()
 
         return carry
 
@@ -417,13 +414,11 @@
 
     @pl.when(core == 1)
     def _():
-        for count in range(DIRECT):
-            wide_copy(2, count, 0).wait_recv()
-        for count in range(9 - DIRECT):
-            wide_copy(3, count, 0).wait_recv()
-        for count in range(SHARED):
-            pair_copy(0, count).wait_recv()
-            pair_copy(1, count).wait_recv()
+        wide_copy(2, UP_RUN, 0).wait_recv()
+        wide_copy(3, DOWN_RUN, 0).wait_recv()
+        for run in PAIR_RUNS:
+            for way in range(2):
+                pair_copy(way, run).wait_recv()
         for step in range(1, COLUMN):
             origin = lax.rem(y + step, COLUMN)
             for tap in range(9):
@@ -433,14 +428,6 @@
             param_copy(step, step).wait_recv()
         pltpu.make_async_copy(weights.at[0], coarse.at[y], local_sem.at[LAYERS]).wait()
         for block in range(COLUMN):
-            center, gain, offset = (params[block, row : row + 1] for row in range(3))
-            source = chain.at[pl.ds(block, 1)]
-            if block == 0:
-                for part in range(HALVES):
-                    hop(part).wait_recv()
-                    activate(source, 1, center, gain, offset, range(part * half, part * half + half))
-            else:
-                activate(source, 1, center, gain, offset)
 
             @pl.when(jnp.logical_or(block != y, y < 2))
             def _():
@@ -452,22 +439,20 @@
                     {"y": block, "core": 1},
                 ).wait_recv()
 
-            if block < COLUMN - 1:
-                increment = convolve(0, lambda tap: coarse[block, tap])
-                chain[block + 1] = chain[block] + COARSE * increment + forcing[block]
-            else:
-                for part in range(HALVES):
-                    first = part * half
-                    taken = pl.ds(first, half)
-                    increment = convolve(0, lambda tap: coarse[block, tap], first, half)
-                    chain[block + 1, taken] = (
-                        chain[block, taken] + COARSE * increment + forcing[block, taken]
-                    )
-
-                    @pl.when(z < planes - 1)
-                    def _():
-                        hop(part).start()
-
+        for part in range(HALVES):
+            hop(part).wait_recv()
+        for block in range(COLUMN):
+            center, gain, offset = (params[block, row : row + 1] for row in range(3))
+            activate(chain.at[pl.ds(block, 1)], 1, center, gain, offset)
+            increment = convolve(0, lambda tap: coarse[block, tap])
+            chain[block + 1] = chain[block] + COARSE * increment + forcing[block]
+
+        @pl.when(z < planes - 1)
+        def _():
+            for part in range(HALVES):
+                hop(part).start()
+
+        for block in range(COLUMN - 1, -1, -1):
             here = (y == block) & (holder == 1)
 
             @pl.when(here)
@@ -515,15 +500,14 @@
 
     @pl.when(core == 1)
     def _():
-        for count in range(DIRECT):
-            wide_copy(0, count, y).wait_send()
-            wide_copy(1, count, y).wait_send()
-            wide_copy(2, count, down).wait_send()
-        for count in range(9 - DIRECT):
-            wide_copy(3, count, up).wait_send()
-        for count in range(SHARED):
-            pair_copy(0, count).wait_send()
-            pair_copy(1, count).wait_send()
+        for run in DIRECT_RUNS:
+            for way in range(2):
+                wide_copy(way, run, y).wait_send()
+        wide_copy(2, UP_RUN, down).wait_send()
+        wide_copy(3, DOWN_RUN, up).wait_send()
+        for run in PAIR_RUNS:
+            for way in range(2):
+                pair_copy(way, run).wait_send()
         for step in range(1, COLUMN):
             param_copy(step, 0).wait_send()
         for block in range(COLUMN):
@@ -571,8 +555,8 @@
             dma((EXCHANGES, peers)),
             dma((2,)),
             dma((2,)),
-            dma((6, DIRECT)),
-            dma((6, DIRECT)),
+            dma((6, 4)),
+            dma((6, 4)),
             dma((samples,)),
             dma((COLUMN,)),
             dma((COLUMN,)),

time: 137 us -> 137 us (level)
  no operation moved by 1% of the time
where the time goes in v4:
time: 137 us; the launch traced here: 135 us
  Pallas kernels  133 us (97%)
  local copies, waits for them, and re-layouts  1.87 us (1%)
    pallas_call x1, Pallas kernels, block_solve(): pl.pallas_call(functools.partial(kernel, planes, chips), out_shape=jax.Sh...  133 us

profile of v4, /device:TPU:229, one launch (start us, length us, event | category | flops | bytes accessed | tf_op | source)
XLA Modules:
  0.0 135.0 jit_solution(7277736248003272995)
XLA Ops:
  0.0 133.1 %shard_map.46 = f32[2,16,16,256]{3,2,1,0:T(8,128)} custom-call(f32[2,16,16,256]{3,2,1,0:T(8,128)} %bitcast.5, bf16[4,3,768,256]{3,2,1,0:T(8,128)(2,1)} %bitcast.3, f32[4,256]{1,0:T(4,128)} %gains.1, f32[4,256]{1,0:T(4,128)} %offsets.1), custom_call_target="tpu_custom_call" | custom-call | tf_op jit(solution)/shard_map/pallas_call | solution.py:530
  133.1 1.9 %copy.6 = f32[1,2,16,16,256]{4,3,2,1,0:T(8,128)} copy(f32[1,2,16,16,256]{4,3,2,1,0:T(8,128)} %bitcast.4) | data formatting | bytes 1048576

commit v5 on v2

--- a/solution.py
+++ b/solution.py
@@ -18,7 +18,7 @@
 EXCHANGES = 8
 EARLY = 7
 RELAYED = 5
-HALVES = 2
+HALVES = 1
 
 
 def remote(src, dst, send_sem, recv_sem, device):
@@ -416,14 +416,6 @@
             param_copy(step, step).wait_recv()
         pltpu.make_async_copy(weights.at[0], coarse.at[y], local_sem.at[LAYERS]).wait()
         for block in range(COLUMN):
-            center, gain, offset = (params[block, row : row + 1] for row in range(3))
-            source = chain.at[pl.ds(block, 1)]
-            if block == 0:
-                for part in range(HALVES):
-                    hop(part).wait_recv()
-                    activate(source, 1, center, gain, offset, range(part * half, part * half + half))
-            else:
-                activate(source, 1, center, gain, offset)
 
             @pl.when(jnp.logical_or(block != y, y < 2))
             def _():
@@ -435,22 +427,20 @@
                     {"y": block, "core": 1},
                 ).wait_recv()
 
-            if block < COLUMN - 1:
-                increment = convolve(0, lambda tap: coarse[block, tap])
-                chain[block + 1] = chain[block] + COARSE * increment + forcing[block]
-            else:
-                for part in range(HALVES):
-                    first = part * half
-                    taken = pl.ds(first, half)
-                    increment = convolve(0, lambda tap: coarse[block, tap], first, half)
-                    chain[block + 1, taken] = (
-                        chain[block, taken] + COARSE * increment + forcing[block, taken]
-                    )
-
-                    @pl.when(z < planes - 1)
-                    def _():
-                        hop(part).start()
-
+        for part in range(HALVES):
+            hop(part).wait_recv()
+        for block in range(COLUMN):
+            center, gain, offset = (params[block, row : row + 1] for row in range(3))
+            activate(chain.at[pl.ds(block, 1)], 1, center, gain, offset)
+            increment = convolve(0, lambda tap: coarse[block, tap])
+            chain[block + 1] = chain[block] + COARSE * increment + forcing[block]
+
+        @pl.when(z < planes - 1)
+        def _():
+            for part in range(HALVES):
+                hop(part).start()
+
+        for block in range(COLUMN - 1, -1, -1):
             here = (y == block) & (holder == 1)
 
             @pl.when(here)

time: 133 us -> 137 us (1.030); the launches traced: 131 us -> 137 us
  Pallas kernels: 129 us -> 135 us
    pallas_call x1, Pallas kernels: 129 us -> 135 us  [block_solve(): pl.pallas_call(functools.partial(kernel, planes, chips), out_shape=jax.Sh...]
where the time goes in v5:
time: 137 us
  Pallas kernels  135 us (99%)
  local copies, waits for them, and re-layouts  1.87 us (1%)
    pallas_call x1, Pallas kernels, block_solve(): pl.pallas_call(functools.partial(kernel, planes, chips), out_shape=jax.Sh...  135 us

profile of v5, /device:TPU:229, one launch (start us, length us, event | category | flops | bytes accessed | tf_op | source)
XLA Modules:
  0.0 137.2 jit_solution(4913637907172113248)
XLA Ops:
  0.0 135.3 %shard_map.46 = f32[2,16,16,256]{3,2,1,0:T(8,128)} custom-call(f32[2,16,16,256]{3,2,1,0:T(8,128)} %bitcast.5, bf16[4,3,768,256]{3,2,1,0:T(8,128)(2,1)} %bitcast.3, f32[4,256]{1,0:T(4,128)} %gains.1, f32[4,256]{1,0:T(4,128)} %offsets.1), custom_call_target="tpu_custom_call" | custom-call | tf_op jit(solution)/shard_map/pallas_call | solution.py:517
  135.3 1.9 %copy.6 = f32[1,2,16,16,256]{4,3,2,1,0:T(8,128)} copy(f32[1,2,16,16,256]{4,3,2,1,0:T(8,128)} %bitcast.4) | data formatting | bytes 1048576

commit v6 on v3

--- a/solution.py
+++ b/solution.py
@@ -252,13 +252,6 @@
             plain, square = plain + folded(value), square + folded(value * value)
         store_sums(layer + 1, plain, square)
         send_sums(layer + 1)
-        for way in range(2):
-
-            @pl.when((core == 1) & (layer == 1 + way))
-            def _():
-                wide_copy(way, 0, y).wait_recv()
-                pair_copy(way, 0).start()
-
         return carry
 
     lax.fori_loop(0, LAYERS, relax, 0)
@@ -269,18 +262,6 @@
     @pl.when(position < final)
     def _():
         relaxed_copy.start()
-
-    @pl.when(core == 1)
-    def _():
-        for count in range(1, DIRECT):
-            for way in range(2):
-                wide_copy(way, count, y).wait_recv()
-                if count < SHARED - 1:
-                    pair_copy(way, count).start()
-        for count in range(DIRECT):
-            wide_copy(2, count, down).start()
-            if count < 9 - DIRECT:
-                wide_copy(3, count, up).start()
 
     passed_sums[0] = gather_sums(LAYERS)
     totals_copy = remote(
@@ -290,6 +271,18 @@
     @pl.when(position < final)
     def _():
         totals_copy.start()
+
+    @pl.when(core == 1)
+    def _():
+        for count in range(DIRECT):
+            wide_copy(0, count, down).wait_recv()
+            wide_copy(2, count, down).start()
+            wide_copy(1, count, up).wait_recv()
+            if count < 9 - DIRECT:
+                wide_copy(3, count, up).start()
+            if count < SHARED // 2:
+                pair_copy(0, count).start()
+                pair_copy(1, count).start()
 
     @pl.when(position > 0)
     def _():
@@ -344,7 +337,7 @@
 
     @pl.when(core == 1)
     def _():
-        pair_copy(0, SHARED - 1).start()
+        pair_copy(0, 2).start()
 
     def refine(layer, carry):
         center, inverse = statistics(gather_sums(LAYERS + layer))
@@ -359,7 +352,12 @@
 
         @pl.when((core == 1) & (layer == 1))
         def _():
-            pair_copy(1, SHARED - 1).start()
+            pair_copy(1, 2).start()
+
+        @pl.when((core == 1) & (layer == 2))
+        def _():
+            for way in range(2):
+                pair_copy(way, 3).start()
 
         return carry
 

time: 137 us -> 122 us (0.89)
  Pallas kernels: 133 us -> 118 us
    pallas_call x1, Pallas kernels: 133 us -> 118 us  [block_solve(): pl.pallas_call(functools.partial(kernel, planes, chips), out_shape=jax.Sh...]
where the time goes in v6:
time: 122 us; the launch traced here: 120 us
  Pallas kernels  118 us (97%)
  local copies, waits for them, and re-layouts  1.87 us (2%)
    pallas_call x1, Pallas kernels, block_solve(): pl.pallas_call(functools.partial(kernel, planes, chips), out_shape=jax.Sh...  118 us

profile of v6, /device:TPU:229, one launch (start us, length us, event | category | flops | bytes accessed | tf_op | source)
XLA Modules:
  0.0 119.8 jit_solution(1659613104171471398)
XLA Ops:
  0.0 117.9 %shard_map.46 = f32[2,16,16,256]{3,2,1,0:T(8,128)} custom-call(f32[2,16,16,256]{3,2,1,0:T(8,128)} %bitcast.5, bf16[4,3,768,256]{3,2,1,0:T(8,128)(2,1)} %bitcast.3, f32[4,256]{1,0:T(4,128)} %gains.1, f32[4,256]{1,0:T(4,128)} %offsets.1), custom_call_target="tpu_custom_call" | custom-call | tf_op jit(solution)/shard_map/pallas_call | solution.py:544
  117.9 1.9 %copy.6 = f32[1,2,16,16,256]{4,3,2,1,0:T(8,128)} copy(f32[1,2,16,16,256]{4,3,2,1,0:T(8,128)} %bitcast.4) | data formatting | bytes 1048576
